TPU v7x, 32 devices: a whole 2x2x4 slice. The times are simulated.
32 devices in a mesh: lat: 4 (over x, core), lon: 4 (over z), lev: 2 (over y).
Axes of the slice: x: 2, y: 2, z: 4, core: 2. Of those that a mesh axis runs over, the one named last changes fastest.
Arguments:
- initial_heat: float32 [128, 512, 8, 128], P('lat', 'lon', 'lev'), may hold values from 0.5 to 2
- diffusivity_ratio: float32 [128, 512, 8, 128], P('lat', 'lon', 'lev'), may hold values from 0.03 to 0.15
- forcing_term: float32 [128, 512, 8, 128], P('lat', 'lon', 'lev'), may hold values from -0.2 to 0.2
Outputs:
- standard_deviation_score: float32 [128, 512, 8, 128], P('lat', 'lon', 'lev')
- temperature_end: float32 [128, 512, 8, 128], P('lat', 'lon', 'lev')
All inputs are finite; a program needn't handle non-finite values.
Results may differ from a plain program's by a relative error of at most 0.00002.
Values sent between devices are 32-bit elements; how exact they have to be, the bound alone decides.
A program may use at most 128 MiB of HBM per device.

v0:
```python
import functools

import jax
import jax.numpy as jnp
from jax import lax
from jax.experimental import pallas as pl
from jax.experimental.pallas import tpu as pltpu
from jax.sharding import PartitionSpec as P

STEPS = 4
PAD = 8
XBLOCK = 32
MESH = pl.DeviceIdType.MESH


def march_kernel(
    sizes, chunks, rows,
    heat_in, ratio_in, forcing_in, raw, moments_out,
    field, ratio, forcing, xsend, xrecv, stats,
    load_heat, load_ratio, load_forcing,
    zsend_sem, zrecv_sem, xsend_sem, xrecv_sem, ysend_sem, yrecv_sem, stat_send, stat_recv,
):
    depth, width, height = sizes
    inner = pl.ds(PAD, width)
    places = {axis: lax.axis_index(axis) for axis in ("lat", "lon", "lev")}
    counts = {axis: lax.axis_size(axis) for axis in ("lat", "lon", "lev")}

    def beside(axis, offset):
        return {axis: lax.rem(places[axis] + offset + counts[axis], counts[axis])}

    def rows_of(c):
        return pl.ds(c * rows, rows)

    def load(c):
        return [
            pltpu.make_async_copy(source.at[rows_of(c)], target.at[rows_of(c)], sem.at[c])
            for source, target, sem in (
                (heat_in, raw, load_heat), (ratio_in, ratio, load_ratio), (forcing_in, forcing, load_forcing),
            )
        ]

    def zcopy(side, p, c):
        span = pl.ds(1 + c * rows, rows)
        return pltpu.make_async_remote_copy(
            src_ref=field.at[p, (1, height)[side], span, inner],
            dst_ref=field.at[p, (height + 1, 0)[side], span, inner],
            send_sem=zsend_sem.at[side, p, c], recv_sem=zrecv_sem.at[1 - side, p, c],
            device_id=beside("lev", (-1, 1)[side]), device_id_type=MESH,
        )

    def xcopy(side, p, c):
        return pltpu.make_async_remote_copy(
            src_ref=xsend.at[side, p, c], dst_ref=xrecv.at[1 - side, p, c],
            send_sem=xsend_sem.at[side, p, c], recv_sem=xrecv_sem.at[1 - side, p, c],
            device_id=beside("lon", (-1, 1)[side]), device_id_type=MESH,
        )

    def ycopy(side, p):
        return pltpu.make_async_remote_copy(
            src_ref=field.at[p, pl.ds(1, height), (1, depth)[side], inner],
            dst_ref=field.at[p, pl.ds(1, height), (depth + 1, 0)[side], inner],
            send_sem=ysend_sem.at[side, p], recv_sem=yrecv_sem.at[1 - side, p],
            device_id=beside("lat", (-1, 1)[side]), device_id_type=MESH,
        )

    def stat_copy(offset, c):
        return pltpu.make_async_remote_copy(
            src_ref=stats.at[0, c], dst_ref=stats.at[offset, c],
            send_sem=stat_send.at[offset - 1, c], recv_sem=stat_recv.at[offset - 1, c],
            device_id=beside("lon", offset), device_id_type=MESH,
        )

    def send(p, c):
        for side, end in ((0, 0), (1, chunks - 1)):
            @pl.when(c == end)
            def _():
                ycopy(side, p).start()
        for side in (0, 1):
            zcopy(side, p, c).start()
        for side in (0, 1):
            xcopy(side, p, c).start()

    def sent(p, c):
        for side, end in ((0, 0), (1, chunks - 1)):
            @pl.when(c == end)
            def _():
                ycopy(side, p).wait_send()
        for side in (0, 1):
            zcopy(side, p, c).wait_send()
            xcopy(side, p, c).wait_send()

    def arrived(p, c):
        for side, end in ((1, 0), (0, chunks - 1)):
            @pl.when(c == end)
            def _():
                ycopy(side, p).wait_recv()
        for side in (0, 1):
            xcopy(side, p, c).wait_recv()
        for side in (0, 1):
            zcopy(side, p, c).wait_recv()

    def pack(p, c, i):
        for z in range(height):
            for side, x in ((0, PAD), (1, PAD + width - 1)):
                xsend[side, p, c, pl.ds(i * height + z, 1), :] = field[p, z + 1, c * rows + i + 1, pl.ds(x, 1), :]

    def start_loads(c, carry):
        load(c)[0].start()
        return carry

    def start_others(c, carry):
        for copy in load(c)[1:]:
            copy.start()
        return carry

    barrier = pltpu.get_barrier_semaphore()
    greeted = [beside("lev", -1), beside("lev", 1), beside("lat", -1), beside("lat", 1)]
    greeted += [beside("lon", offset) for offset in range(1, counts["lon"])]
    for device in greeted:
        pl.semaphore_signal(barrier, inc=1, device_id=device, device_id_type=MESH)
    lax.fori_loop(0, chunks, start_loads, 0)

    def unpack(c):
        load(c)[0].wait()

        def row(i, carry):
            y = c * rows + i
            for z in range(height):
                field[0, z + 1, y + 1, inner, :] = raw[y, pl.ds(z, width, stride=height), :]
            pack(0, c, i)
            return carry

        lax.fori_loop(0, rows, row, 0)

    def unpack_send(c, carry):
        unpack(c)
        send(0, c)
        return carry

    unpack(0)
    pl.semaphore_wait(barrier, len(greeted))
    send(0, 0)
    lax.fori_loop(0, chunks, start_others, 0)
    lax.fori_loop(1, chunks, unpack_send, 0)

    def combine(c):
        for offset in range(1, counts["lon"]):
            stat_copy(offset, c).wait_recv()
        means = [stats[offset, c, 0] for offset in range(counts["lon"])]
        mean = sum(means[1:], means[0]) * (1.0 / counts["lon"])
        squares = sum([stats[offset, c, 1] for offset in range(1, counts["lon"])], stats[0, c, 1])
        apart = sum([(other - mean) * (other - mean) for other in means[1:]], (means[0] - mean) * (means[0] - mean))
        variance = (squares + width * apart) * (1.0 / (width * counts["lon"]))
        scale = lax.rsqrt(variance + 0.0001)
        for i in range(rows):
            for half in range(2):
                for kind, values in ((0, mean), (1, scale)):
                    moments_out[kind, c * rows + i, pl.ds(half * height, height), :] = values[i * height:(i + 1) * height]
        for offset in range(1, counts["lon"]):
            stat_copy(offset, c).wait_send()
        sent((STEPS - 1) % 2, c)

    def step(s, carry):
        p = lax.rem(s, 2)
        q = 1 - p

        def chunk(c, carry):
            @pl.when(s == 0)
            def _():
                for copy in load(c)[1:]:
                    copy.wait()

            @pl.when(s >= 1)
            def _():
                sent(q, c)

            arrived(p, c)

            def row(i, carry):
                y = c * rows + i
                for z in range(height):
                    for side, x in ((0, PAD - 1), (1, PAD + width)):
                        field[p, z + 1, y + 1, pl.ds(x, 1), :] = xrecv[side, p, c, pl.ds(i * height + z, 1), :]
                for x in range(0, width, XBLOCK):
                    here = pl.ds(PAD + x, XBLOCK)
                    planes = [field[p, z, y + 1, here, :] for z in range(height + 2)]
                    for z in range(height):
                        middle = planes[z + 1]
                        spread = (
                            field[p, z + 1, y, here, :] + field[p, z + 1, y + 2, here, :]
                            + field[p, z + 1, y + 1, pl.ds(PAD + x - 1, XBLOCK), :]
                            + field[p, z + 1, y + 1, pl.ds(PAD + x + 1, XBLOCK), :]
                            + planes[z] + planes[z + 2] - 6.0 * middle
                        )
                        cells = pl.ds(x * height + z, XBLOCK, stride=height)
                        field[q, z + 1, y + 1, here, :] = middle + ratio[y, cells, :] * spread + forcing[y, cells, :]
                pack(q, c, i)
                return carry

            lax.fori_loop(0, rows, row, 0)

            @pl.when(s < STEPS - 1)
            def _():
                send(q, c)

            @pl.when(s == STEPS - 1)
            def _():
                def finish(i, carry):
                    y = c * rows + i
                    for z in range(height):
                        line = field[q, z + 1, y + 1, inner, :]
                        raw[y, pl.ds(z, width, stride=height), :] = line
                        mean = jnp.sum(line, axis=0, keepdims=True) * (1.0 / width)
                        centred = line - mean
                        stats[0, c, 0, pl.ds(i * height + z, 1), :] = mean
                        stats[0, c, 1, pl.ds(i * height + z, 1), :] = jnp.sum(centred * centred, axis=0, keepdims=True)
                    return carry

                lax.fori_loop(0, rows, finish, 0)
                for offset in range(1, counts["lon"]):
                    stat_copy(offset, c).start()

                @pl.when(c >= 1)
                def _():
                    combine(c - 1)

            return carry

        lax.fori_loop(0, chunks, chunk, 0)
        return carry

    lax.fori_loop(0, STEPS, step, 0)


    combine(chunks - 1)


def score_kernel(chunks, heat, moments, score, end, scaled, score_sem, end_sem):
    rows = heat.shape[0] // chunks
    finish = pltpu.make_async_copy(heat, end, end_sem)
    finish.start()

    def out_copy(c):
        span = pl.ds(c * rows, rows)
        return pltpu.make_async_copy(scaled.at[span], score.at[span], score_sem.at[c])

    def chunk(c, carry):
        def row(i, carry):
            y = c * rows + i
            mean, scale = moments[0, y], moments[1, y]
            values = heat[y]
            tall = values.reshape(values.shape[0] // mean.shape[0], *mean.shape)
            scaled[y] = ((tall - mean[None]) * scale[None]).reshape(values.shape)
            return carry

        lax.fori_loop(0, rows, row, 0)
        out_copy(c).start()
        return carry

    def drain(c, carry):
        out_copy(c).wait()
        return carry

    lax.fori_loop(0, chunks, chunk, 0)
    lax.fori_loop(0, chunks, drain, 0)
    finish.wait()


def local(initial_heat, diffusivity_ratio, forcing_term):
    depth, width, height, members = initial_heat.shape
    rows = 2
    chunks = depth // rows
    lon = lax.axis_size("lon")
    flat = (depth, width * height, members)
    f32 = jnp.float32
    anywhere = pl.BlockSpec(memory_space=pl.ANY)
    dma = pltpu.SemaphoreType.DMA
    heat, moments = pl.pallas_call(
        functools.partial(march_kernel, (depth, width, height), chunks, rows),
        out_shape=(pltpu.VMEM(flat, f32), pltpu.VMEM((2, depth, 2 * height, members), f32)),
        in_specs=[anywhere] * 3,
        out_specs=(pl.BlockSpec(memory_space=pltpu.VMEM),) * 2,
        scratch_shapes=[
            pltpu.VMEM((2, height + 2, depth + 2, width + 2 * PAD, members), f32),
            pltpu.VMEM(flat, f32),
            pltpu.VMEM(flat, f32),
            pltpu.VMEM((2, 2, chunks, rows * height, members), f32),
            pltpu.VMEM((2, 2, chunks, rows * height, members), f32),
            pltpu.VMEM((lon, chunks, 2, rows * height, members), f32),
            dma((chunks,)), dma((chunks,)), dma((chunks,)),
            dma((2, 2, chunks)), dma((2, 2, chunks)),
            dma((2, 2, chunks)), dma((2, 2, chunks)),
            dma((2, 2)), dma((2, 2)),
            dma((lon - 1, chunks)), dma((lon - 1, chunks)),
        ],
        compiler_params=pltpu.CompilerParams(
            collective_id=0, has_side_effects=True, vmem_limit_bytes=48 * 1024 * 1024
        ),
        name="march",
    )(*[a.reshape(flat) for a in (initial_heat, diffusivity_ratio, forcing_term)])
    parts = min(8, depth)
    score, end = pl.pallas_call(
        functools.partial(score_kernel, parts),
        out_shape=(jax.ShapeDtypeStruct(flat, f32),) * 2,
        in_specs=[pl.BlockSpec(memory_space=pltpu.VMEM)] * 2,
        out_specs=(anywhere,) * 2,
        scratch_shapes=[pltpu.VMEM(flat, f32), dma((parts,)), dma(())],
        compiler_params=pltpu.CompilerParams(vmem_limit_bytes=24 * 1024 * 1024),
        name="score",
    )(heat, moments)
    return score.reshape(initial_heat.shape), end.reshape(initial_heat.shape)


def solution(mesh):
    placed = P("lat", "lon", "lev", None)
    return jax.shard_map(
        local, mesh=mesh, in_specs=(placed,) * 3, out_specs=(placed,) * 2, check_vma=False
    )
```

profile of v0, /device:TPU:0, one launch (start us, length us, event | category | flops | bytes accessed | tf_op | source)
XLA Modules:
  0.0 381.2 jit_solution(18259378295340425151)
XLA Ops:
  0.6 374.5 %march.1 = (f32[32,512,128]{2,1,0:T(8,128)S(1)}, f32[2,32,8,128]{3,2,1,0:T(8,128)S(1)}) custom-call(f32[32,512,128]{2,1,0:T(8,128)} %bitcast.5, f32[32,512,128]{2,1,0:T(8,128)} %bitcast.6, f32[32,512,128]{2,1,0:T(8,128)} %bitcast.7), custom_call_target="tpu_custom_call" | custom-call | tf_op jit(solution)/shard_map/march/pallas_call | solution.py:278
  375.2 6.0 %score.1 = (f32[32,512,128]{2,1,0:T(8,128)}, f32[32,512,128]{2,1,0:T(8,128)}) custom-call(f32[32,512,128]{2,1,0:T(8,128)S(1)} %get-tuple-element.6.heat, f32[2,32,8,128]{3,2,1,0:T(8,128)S(1)} %get-tuple-element.7.moments), custom_call_target="tpu_custom_call" | custom-call | tf_op jit(solution)/shard_map/score/pallas_call | solution.py:302
where the time goes:
time: 381 us
  Pallas kernels  381 us (100%)
    pallas_call x1, Pallas kernels, local(): pl.pallas_call(functools.partial(march_kernel, (depth, width, height), ch...  375 us

commit v1 on v0

--- a/solution.py
+++ b/solution.py
@@ -10,6 +10,7 @@
 STEPS = 4
 PAD = 8
 XBLOCK = 32
+XCELLS = 16
 MESH = pl.DeviceIdType.MESH
 
 
@@ -235,39 +236,454 @@
     combine(chunks - 1)
 
 
-def score_kernel(chunks, heat, moments, score, end, scaled, score_sem, end_sem):
-    rows = heat.shape[0] // chunks
-    finish = pltpu.make_async_copy(heat, end, end_sem)
-    finish.start()
-
-    def out_copy(c):
-        span = pl.ds(c * rows, rows)
-        return pltpu.make_async_copy(scaled.at[span], score.at[span], score_sem.at[c])
-
-    def chunk(c, carry):
-        def row(i, carry):
+def swap_kernel(
+    sizes, rows,
+    heat_in, ratio_in, forcing_in, heat_out, moments_out,
+    field, rim, core, ratio, ratio_far, forcing_far, back, stage,
+    xsend, xrecv, csend, crecv, stats,
+    load_sem, r_send, r_recv, u_send, u_recv, f_send, f_recv, b_send, b_recv,
+    xsend_sem, xrecv_sem, ysend_sem, yrecv_sem, cxsend_sem, cxrecv_sem, cysend_sem, cyrecv_sem,
+    stat_send, stat_recv,
+):
+    depth, width, height = sizes
+    half, planes, inside = width // 2, 2 * height, height - 2
+    chunks = depth // rows
+    units = chunks // 2
+    sent_at = height * half
+    inner = pl.ds(PAD, half)
+    forcing = heat_out
+    places = {axis: lax.axis_index(axis) for axis in ("lat", "lon", "lev")}
+    counts = {axis: lax.axis_size(axis) for axis in ("lat", "lon", "lev")}
+    upper = places["lev"] == 1
+
+    def beside(axis, offset):
+        return {axis: lax.rem(places[axis] + offset + counts[axis], counts[axis])}
+
+    def rows_of(c):
+        return pl.ds(c * rows, rows)
+
+    def chunk_of(u, side):
+        return u + side * (chunks - 1 - 2 * u)
+
+    def first_lanes(shape):
+        return lax.broadcasted_iota(jnp.int32, shape, 1) < shape[1] // 2
+
+    def turned(values):
+        return pltpu.roll(values, values.shape[1] // 2, 1)
+
+    def remote(source, target, send_sem, recv_sem, device):
+        return pltpu.make_async_remote_copy(
+            src_ref=source, dst_ref=target, send_sem=send_sem, recv_sem=recv_sem,
+            device_id=device, device_id_type=MESH,
+        )
+
+    partner = beside("lev", 1)
+
+    def load(kind, c, slot):
+        source = (heat_in, ratio_in, forcing_in)[kind]
+        return pltpu.make_async_copy(source.at[rows_of(c)], stage.at[kind, slot], load_sem.at[kind, slot])
+
+    def ratio_copy(c):
+        return remote(
+            ratio.at[rows_of(c), pl.ds(sent_at, sent_at)], ratio_far.at[rows_of(c)], r_send.at[c], r_recv.at[c], partner
+        )
+
+    def forcing_copy(c):
+        return remote(
+            forcing.at[rows_of(c), pl.ds(sent_at, sent_at)], forcing_far.at[rows_of(c)], f_send.at[c], f_recv.at[c], partner
+        )
+
+    def rim_copy(end, c):
+        return remote(
+            rim.at[end, rows_of(c)], field.at[0, (height, planes - 1)[end], pl.ds(1 + c * rows, rows), inner],
+            u_send.at[end, c], u_recv.at[end, c], partner,
+        )
+
+    def back_copy(c):
+        return remote(
+            field.at[STEPS % 2, pl.ds(height, height), pl.ds(1 + c * rows, rows), inner], back.at[:, rows_of(c)],
+            b_send.at[c], b_recv.at[c], partner,
+        )
+
+    def xcopy(level, side, c):
+        return remote(
+            xsend.at[level, side, rows_of(c)], xrecv.at[level, 1 - side, rows_of(c)],
+            xsend_sem.at[level, side, c], xrecv_sem.at[level, 1 - side, c], beside("lon", (-1, 1)[side]),
+        )
+
+    def ycopy(level, side):
+        p = lax.rem(level, 2)
+        return remote(
+            field.at[p, :, (1, depth)[side], inner], field.at[p, :, (depth + 1, 0)[side], inner],
+            ysend_sem.at[level, side], yrecv_sem.at[level, 1 - side], beside("lat", (-1, 1)[side]),
+        )
+
+    def core_xcopy(side, c):
+        return remote(
+            csend.at[side, rows_of(c)], crecv.at[1 - side, rows_of(c)],
+            cxsend_sem.at[side, c], cxrecv_sem.at[1 - side, c], beside("lon", (-1, 1)[side]),
+        )
+
+    def core_ycopy(side):
+        return remote(
+            core.at[:, (1, depth)[side], inner], core.at[:, (depth + 1, 0)[side], inner],
+            cysend_sem.at[side], cyrecv_sem.at[1 - side], beside("lat", (-1, 1)[side]),
+        )
+
+    def stat_copy(offset, c):
+        return remote(
+            stats.at[0, c], stats.at[offset, c], stat_send.at[offset - 1, c], stat_recv.at[offset - 1, c],
+            beside("lon", offset),
+        )
+
+    def at_ends(c, action):
+        for side, end in ((0, 0), (1, chunks - 1)):
+            @pl.when(c == end)
+            def _():
+                action(side)
+
+    def over(count, body):
+        def step(i, carry):
+            body(i)
+            return carry
+
+        lax.fori_loop(0, count, step, 0)
+
+
+    def split(kind, slot, i, z, x):
+        low = stage[kind, slot, i, pl.ds(x * height + z, XBLOCK, stride=height), :]
+        high = stage[kind, slot, i, pl.ds((half + x) * height + z, XBLOCK, stride=height), :]
+        mask = first_lanes(low.shape)
+        one = jnp.where(mask, low, turned(high))
+        two = jnp.where(mask, turned(low), high)
+        return jnp.where(upper, two, one), jnp.where(upper, one, two)
+
+    def split_into(target, kind, slot, c):
+        def row(i):
+            for z in range(height):
+                for x in range(0, half, XBLOCK):
+                    kept, sent = split(kind, slot, i, z, x)
+                    target[c * rows + i, pl.ds(z * half + x, XBLOCK), :] = kept
+                    target[c * rows + i, pl.ds(sent_at + z * half + x, XBLOCK), :] = sent
+
+        over(rows, row)
+
+    def split_heat(slot, c):
+        def row(i):
             y = c * rows + i
-            mean, scale = moments[0, y], moments[1, y]
-            values = heat[y]
-            tall = values.reshape(values.shape[0] // mean.shape[0], *mean.shape)
-            scaled[y] = ((tall - mean[None]) * scale[None]).reshape(values.shape)
-            return carry
-
-        lax.fori_loop(0, rows, row, 0)
-        out_copy(c).start()
-        return carry
-
-    def drain(c, carry):
-        out_copy(c).wait()
-        return carry
-
-    lax.fori_loop(0, chunks, chunk, 0)
-    lax.fori_loop(0, chunks, drain, 0)
-    finish.wait()
-
-
-def local(initial_heat, diffusivity_ratio, forcing_term):
-    depth, width, height, members = initial_heat.shape
+            for z in range(height):
+                for x in range(0, half, XBLOCK):
+                    here = pl.ds(PAD + x, XBLOCK)
+                    kept, sent = split(0, slot, i, z, x)
+                    field[0, z, y + 1, here, :] = kept
+                    if 0 < z < height - 1:
+                        core[z - 1, y + 1, here, :] = sent
+                        field[0, height + z, y + 1, here, :] = jnp.zeros_like(sent)
+                    else:
+                        rim[min(z, 1), y, pl.ds(x, XBLOCK), :] = sent
+            for side, x in ((0, PAD), (1, PAD + half - 1)):
+                csend[side, y] = jnp.zeros(csend.shape[2:], csend.dtype)
+                for n in range(inside):
+                    csend[side, y, pl.ds(n, 1), :] = core[n, y + 1, pl.ds(x, 1), :]
+
+        over(rows, row)
+
+    def prepare(u, side):
+        c = chunk_of(u, side)
+        load(1, c, side).wait()
+        split_into(ratio, 1, side, c)
+
+        @pl.when((u == 0) & (side == 0))
+        def _():
+            pl.semaphore_wait(barrier, len(greeted))
+
+        ratio_copy(c).start()
+        load(0, c, side).wait()
+        split_heat(side, c)
+        for end in (0, 1):
+            rim_copy(end, c).start()
+        for end in (0, 1):
+            core_xcopy(end, c).start()
+        at_ends(c, lambda end: core_ycopy(end).start())
+        load(2, c, side).wait()
+        split_into(forcing, 2, side, c)
+
+        @pl.when(u < units - 1)
+        def _():
+            for kind in (1, 0, 2):
+                load(kind, chunk_of(u + 1, side), side).start()
+
+    def correct(u, side):
+        c = chunk_of(u, side)
+        at_ends(c, lambda end: core_ycopy(1 - end).wait_recv())
+        for end in (0, 1):
+            core_xcopy(end, c).wait_recv()
+
+        def row(i):
+            y = c * rows + i
+            mask = first_lanes(crecv.shape[2:])
+            left = turned(jnp.where(mask, csend[1, y], crecv[0, y]))
+            right = turned(jnp.where(mask, crecv[1, y], csend[0, y]))
+            for n in range(inside):
+                core[n, y + 1, pl.ds(PAD - 1, 1), :] = left[n:n + 1]
+                core[n, y + 1, pl.ds(PAD + half, 1), :] = right[n:n + 1]
+            for x in range(0, half, XBLOCK):
+                here = pl.ds(PAD + x, XBLOCK)
+                middles = {n: core[n, y + 1, here, :] for n in range(inside)}
+                for z in range(height):
+                    parts = [middles[n] for n in (z - 2, z) if n in middles]
+                    n = z - 1
+                    if n in middles:
+                        parts += [
+                            core[n, y, here, :] + core[n, y + 2, here, :],
+                            core[n, y + 1, pl.ds(PAD + x - 1, XBLOCK), :] + core[n, y + 1, pl.ds(PAD + x + 1, XBLOCK), :],
+                            -6.0 * middles[n],
+                        ]
+                    cells = pl.ds(sent_at + z * half + x, XBLOCK)
+                    forcing[y, cells, :] = forcing[y, cells, :] + ratio[y, cells, :] * sum(parts[1:], parts[0])
+
+        over(rows, row)
+        forcing_copy(c).start()
+
+    barrier = pltpu.get_barrier_semaphore()
+    greeted = [partner, beside("lat", -1), beside("lat", 1)]
+    greeted += [beside("lon", offset) for offset in range(1, counts["lon"])]
+    for device in greeted:
+        pl.semaphore_signal(barrier, inc=1, device_id=device, device_id_type=MESH)
+    for side in (0, 1):
+        for kind in (1, 0, 2):
+            load(kind, chunk_of(0, side), side).start()
+
+    def inputs(u):
+        @pl.when(u < units)
+        def _():
+            over(2, lambda side: prepare(u, side))
+
+        @pl.when(u > 0)
+        def _():
+            over(2, lambda side: correct(u - 1, side))
+
+    over(units + 1, inputs)
+
+
+    def publish(level, c):
+        p = lax.rem(level, 2)
+
+        def row(i):
+            y = c * rows + i
+            for side, x in ((0, PAD), (1, PAD + half - 1)):
+                for z in range(planes):
+                    xsend[level, side, y, pl.ds(z, 1), :] = field[p, z, y + 1, pl.ds(x, 1), :]
+
+        over(rows, row)
+        for side in (0, 1):
+            xcopy(level, side, c).start()
+        at_ends(c, lambda side: ycopy(level, side).start())
+
+    def arrive(u, side):
+        c = chunk_of(u, side)
+        ratio_copy(c).wait_recv()
+        forcing_copy(c).wait_recv()
+        for end in (0, 1):
+            rim_copy(end, c).wait_recv()
+        publish(0, c)
+
+    def advance(s, u, side):
+        c = chunk_of(u, side)
+        level = s - 1
+        p = lax.rem(level, 2)
+        q = 1 - p
+        at_ends(c, lambda end: ycopy(level, 1 - end).wait_recv())
+
+        @pl.when(s >= 2)
+        def _():
+            at_ends(c, lambda end: ycopy(s - 2, end).wait_send())
+
+        for end in (0, 1):
+            xcopy(level, end, c).wait_recv()
+
+        def row(i):
+            y = c * rows + i
+            mask = first_lanes(xrecv.shape[3:])
+            left = turned(jnp.where(mask, xsend[level, 1, y], xrecv[level, 0, y]))
+            right = turned(jnp.where(mask, xrecv[level, 1, y], xsend[level, 0, y]))
+            for z in range(planes):
+                field[p, z, y + 1, pl.ds(PAD - 1, 1), :] = left[z:z + 1]
+                field[p, z, y + 1, pl.ds(PAD + half, 1), :] = right[z:z + 1]
+            for x in range(0, half, XCELLS):
+                here = pl.ds(PAD + x, XCELLS)
+                middles = [field[p, z, y + 1, here, :] for z in range(planes)]
+                for z in range(planes):
+                    middle = middles[z]
+                    spread = (
+                        field[p, z, y, here, :] + field[p, z, y + 2, here, :]
+                        + field[p, z, y + 1, pl.ds(PAD + x - 1, XCELLS), :]
+                        + field[p, z, y + 1, pl.ds(PAD + x + 1, XCELLS), :]
+                        + middles[z - 1] + middles[(z + 1) % planes]
+                        - 6.0 * middle
+                    )
+                    if z < height:
+                        cells = pl.ds(z * half + x, XCELLS)
+                        scale, source = ratio[y, cells, :], forcing[y, cells, :]
+                    else:
+                        cells = pl.ds((z - height) * half + x, XCELLS)
+                        scale, source = ratio_far[y, cells, :], forcing_far[y, cells, :]
+                    field[q, z, y + 1, here, :] = middle + scale * spread + source
+
+        over(rows, row)
+
+        @pl.when(s < STEPS)
+        def _():
+            publish(s, c)
+
+        @pl.when(s == STEPS)
+        def _():
+            back_copy(c).start()
+
+    def wave(w):
+        @pl.when(w < units)
+        def _():
+            over(2, lambda side: arrive(w, side))
+
+        def step(i):
+            u = w - 1 - i
+
+            @pl.when((u >= 0) & (u < units))
+            def _():
+                over(2, lambda side: advance(i + 1, u, side))
+
+        over(STEPS, step)
+
+    over(units + STEPS, wave)
+
+
+    def finish(c):
+        back_copy(c).wait_recv()
+        forcing_copy(c).wait_send()
+
+        def row(i):
+            y = c * rows + i
+            for z in range(height):
+                parts = []
+                for x in range(0, half, XBLOCK):
+                    here = pl.ds(PAD + x, XBLOCK)
+                    kept, other = field[STEPS % 2, z, y + 1, here, :], back[z, y, pl.ds(x, XBLOCK), :]
+                    if 0 < z < height - 1:
+                        other = other + core[z - 1, y + 1, here, :]
+                    mask = first_lanes(kept.shape)
+                    one, two = jnp.where(upper, other, kept), jnp.where(upper, kept, other)
+                    low = jnp.where(mask, one, turned(two))
+                    high = jnp.where(mask, turned(one), two)
+                    heat_out[y, pl.ds(x * height + z, XBLOCK, stride=height), :] = low
+                    heat_out[y, pl.ds((half + x) * height + z, XBLOCK, stride=height), :] = high
+                    parts += [low, high]
+                line = jnp.concatenate(parts, axis=0)
+                mean = jnp.sum(line, axis=0, keepdims=True) * (1.0 / width)
+                centred = line - mean
+                stats[0, c, 0, pl.ds(i * height + z, 1), :] = mean
+                stats[0, c, 1, pl.ds(i * height + z, 1), :] = jnp.sum(centred * centred, axis=0, keepdims=True)
+
+        over(rows, row)
+        for offset in range(1, counts["lon"]):
+            stat_copy(offset, c).start()
+
+    def combine(c):
+        for offset in range(1, counts["lon"]):
+            stat_copy(offset, c).wait_recv()
+        means = [stats[offset, c, 0] for offset in range(counts["lon"])]
+        mean = sum(means[1:], means[0]) * (1.0 / counts["lon"])
+        squares = sum([stats[offset, c, 1] for offset in range(1, counts["lon"])], stats[0, c, 1])
+        apart = sum([(other - mean) * (other - mean) for other in means[1:]], (means[0] - mean) * (means[0] - mean))
+        variance = (squares + width * apart) * (1.0 / (width * counts["lon"]))
+        scale = lax.rsqrt(variance + 0.0001)
+        for i in range(rows):
+            for copy in range(2):
+                for kind, values in ((0, mean), (1, scale)):
+                    moments_out[kind, c * rows + i, pl.ds(copy * height, height), :] = values[i * height:(i + 1) * height]
+        for offset in range(1, counts["lon"]):
+            stat_copy(offset, c).wait_send()
+
+    def ordered(i):
+        return chunk_of(i // 2, lax.rem(i, 2))
+
+    def ending(i):
+        finish(ordered(i))
+
+        @pl.when(i > 0)
+        def _():
+            combine(ordered(i - 1))
+
+    over(chunks, ending)
+
+    def drain(c):
+        ratio_copy(c).wait_send()
+        back_copy(c).wait_send()
+        for side in (0, 1):
+            rim_copy(side, c).wait_send()
+            core_xcopy(side, c).wait_send()
+
+        def level_sent(level):
+            for side in (0, 1):
+                xcopy(level, side, c).wait_send()
+
+        over(STEPS, level_sent)
+
+    over(chunks, drain)
+    for side in (0, 1):
+        core_ycopy(side).wait_send()
+        ycopy(STEPS - 1, side).wait_send()
+    combine(ordered(chunks - 1))
+
+
+def swap(sizes, arrays):
+    depth, width, height = sizes
+    members = arrays[0].shape[-1]
+    rows = 2
+    chunks = depth // rows
+    half = width // 2
+    lon = lax.axis_size("lon")
+    flat = (depth, width * height, members)
+    f32 = jnp.float32
+    dma = pltpu.SemaphoreType.DMA
+    vmem = lambda *shape: pltpu.VMEM((*shape, members), f32)
+    return pl.pallas_call(
+        functools.partial(swap_kernel, sizes, rows),
+        out_shape=(pltpu.VMEM(flat, f32), pltpu.VMEM((2, depth, 2 * height, members), f32)),
+        in_specs=[pl.BlockSpec(memory_space=pl.ANY)] * 3,
+        out_specs=(pl.BlockSpec(memory_space=pltpu.VMEM),) * 2,
+        scratch_shapes=[
+            vmem(2, 2 * height, depth + 2, half + 2 * PAD),
+            vmem(2, depth, half),
+            vmem(height - 2, depth + 2, half + 2 * PAD),
+            vmem(depth, width * height),
+            vmem(depth, half * height),
+            vmem(depth, half * height),
+            vmem(height, depth, half),
+            vmem(3, 2, rows, width * height),
+            vmem(STEPS, 2, depth, 2 * height), vmem(STEPS, 2, depth, 2 * height),
+            vmem(2, depth, 8), vmem(2, depth, 8),
+            vmem(lon, chunks, 2, rows * height),
+            dma((3, 2)),
+            dma((chunks,)), dma((chunks,)),
+            dma((2, chunks)), dma((2, chunks)),
+            dma((chunks,)), dma((chunks,)),
+            dma((chunks,)), dma((chunks,)),
+            dma((STEPS, 2, chunks)), dma((STEPS, 2, chunks)),
+            dma((STEPS, 2)), dma((STEPS, 2)),
+            dma((2, chunks)), dma((2, chunks)),
+            dma((2,)), dma((2,)),
+            dma((lon - 1, chunks)), dma((lon - 1, chunks)),
+        ],
+        compiler_params=pltpu.CompilerParams(
+            collective_id=1, has_side_effects=True, vmem_limit_bytes=54 * 1024 * 1024
+        ),
+        name="swap",
+    )(*arrays)
+
+
+def march(sizes, arrays):
+    depth, width, height = sizes
+    members = arrays[0].shape[-1]
     rows = 2
     chunks = depth // rows
     lon = lax.axis_size("lon")
@@ -275,7 +691,7 @@
     f32 = jnp.float32
     anywhere = pl.BlockSpec(memory_space=pl.ANY)
     dma = pltpu.SemaphoreType.DMA
-    heat, moments = pl.pallas_call(
+    return pl.pallas_call(
         functools.partial(march_kernel, (depth, width, height), chunks, rows),
         out_shape=(pltpu.VMEM(flat, f32), pltpu.VMEM((2, depth, 2 * height, members), f32)),
         in_specs=[anywhere] * 3,
@@ -297,7 +713,50 @@
             collective_id=0, has_side_effects=True, vmem_limit_bytes=48 * 1024 * 1024
         ),
         name="march",
-    )(*[a.reshape(flat) for a in (initial_heat, diffusivity_ratio, forcing_term)])
+    )(*arrays)
+
+
+def score_kernel(chunks, heat, moments, score, end, scaled, score_sem, end_sem):
+    rows = heat.shape[0] // chunks
+    finish = pltpu.make_async_copy(heat, end, end_sem)
+    finish.start()
+
+    def out_copy(c):
+        span = pl.ds(c * rows, rows)
+        return pltpu.make_async_copy(scaled.at[span], score.at[span], score_sem.at[c])
+
+    def chunk(c, carry):
+        def row(i, carry):
+            y = c * rows + i
+            mean, scale = moments[0, y], moments[1, y]
+            values = heat[y]
+            tall = values.reshape(values.shape[0] // mean.shape[0], *mean.shape)
+            scaled[y] = ((tall - mean[None]) * scale[None]).reshape(values.shape)
+            return carry
+
+        lax.fori_loop(0, rows, row, 0)
+        out_copy(c).start()
+        return carry
+
+    def drain(c, carry):
+        out_copy(c).wait()
+        return carry
+
+    lax.fori_loop(0, chunks, chunk, 0)
+    lax.fori_loop(0, chunks, drain, 0)
+    finish.wait()
+
+
+def local(initial_heat, diffusivity_ratio, forcing_term):
+    depth, width, height, members = initial_heat.shape
+    flat = (depth, width * height, members)
+    f32 = jnp.float32
+    anywhere = pl.BlockSpec(memory_space=pl.ANY)
+    dma = pltpu.SemaphoreType.DMA
+    arrays = [a.reshape(flat) for a in (initial_heat, diffusivity_ratio, forcing_term)]
+    swaps = lax.axis_size("lev") == 2 and 3 <= height and 3 * height + 2 < 4 * STEPS
+    swaps = swaps and depth % 4 == 0 and width % (2 * XBLOCK) == 0
+    heat, moments = (swap if swaps else march)((depth, width, height), arrays)
     parts = min(8, depth)
     score, end = pl.pallas_call(
         functools.partial(score_kernel, parts),

time: 381 us -> 338 us (0.89)
  Pallas kernels: 381 us -> 337 us
    pallas_call x1, Pallas kernels: 375 us -> 331 us  [swap(): pl.pallas_call(functools.partial(swap_kernel, sizes, rows), out_shape=(pl...]
where the time goes in v1:
time: 338 us
  Pallas kernels  337 us (100%)
    pallas_call x1, Pallas kernels, swap(): pl.pallas_call(functools.partial(swap_kernel, sizes, rows), out_shape=(pl...  331 us

profile of v1, /device:TPU:0, one launch (start us, length us, event | category | flops | bytes accessed | tf_op | source)
XLA Modules:
  0.0 337.8 jit_solution(16758662787483252869)
XLA Ops:
  0.6 331.1 %swap.1 = (f32[32,512,128]{2,1,0:T(8,128)S(1)}, f32[2,32,8,128]{3,2,1,0:T(8,128)S(1)}) custom-call(f32[32,512,128]{2,1,0:T(8,128)} %bitcast.5, f32[32,512,128]{2,1,0:T(8,128)} %bitcast.6, f32[32,512,128]{2,1,0:T(8,128)} %bitcast.7), custom_call_target="tpu_custom_call" | custom-call | tf_op jit(solution)/shard_map/swap/pallas_call | solution.py:649
  331.7 6.0 %score.1 = (f32[32,512,128]{2,1,0:T(8,128)}, f32[32,512,128]{2,1,0:T(8,128)}) custom-call(f32[32,512,128]{2,1,0:T(8,128)S(1)} %get-tuple-element.6.heat, f32[2,32,8,128]{3,2,1,0:T(8,128)S(1)} %get-tuple-element.7.moments), custom_call_target="tpu_custom_call" | custom-call | tf_op jit(solution)/shard_map/score/pallas_call | solution.py:761

commit v2 on v1

--- a/solution.py
+++ b/solution.py
@@ -238,12 +238,11 @@
 
 def swap_kernel(
     sizes, rows,
-    heat_in, ratio_in, forcing_in, heat_out, moments_out,
-    field, rim, core, ratio, ratio_far, forcing_far, back, stage,
+    heat_in, ratio_in, forcing_in, heat_out, score_out,
+    field, rim, core, ratio_far, forcing_far, back, stage,
     xsend, xrecv, csend, crecv, stats,
-    load_sem, r_send, r_recv, u_send, u_recv, f_send, f_recv, b_send, b_recv,
-    xsend_sem, xrecv_sem, ysend_sem, yrecv_sem, cxsend_sem, cxrecv_sem, cysend_sem, cyrecv_sem,
-    stat_send, stat_recv,
+    load_sem, send_sem, ysend_sem, scale_recv, rim_recv, back_recv,
+    xrecv_sem, yrecv_sem, cxrecv_sem, cyrecv_sem, stat_recv,
 ):
     depth, width, height = sizes
     half, planes, inside = width // 2, 2 * height, height - 2
@@ -251,7 +250,7 @@
     units = chunks // 2
     sent_at = height * half
     inner = pl.ds(PAD, half)
-    forcing = heat_out
+    forcing, ratio = heat_out, score_out
     places = {axis: lax.axis_index(axis) for axis in ("lat", "lon", "lev")}
     counts = {axis: lax.axis_size(axis) for axis in ("lat", "lon", "lev")}
     upper = places["lev"] == 1
@@ -267,6 +266,9 @@
 
     def first_lanes(shape):
         return lax.broadcasted_iota(jnp.int32, shape, 1) < shape[1] // 2
+
+    def ordered(i):
+        return chunk_of(i // 2, lax.rem(i, 2))
 
     def turned(values):
         return pltpu.roll(values, values.shape[1] // 2, 1)
@@ -283,64 +285,58 @@
         source = (heat_in, ratio_in, forcing_in)[kind]
         return pltpu.make_async_copy(source.at[rows_of(c)], stage.at[kind, slot], load_sem.at[kind, slot])
 
-    def ratio_copy(c):
-        return remote(
-            ratio.at[rows_of(c), pl.ds(sent_at, sent_at)], ratio_far.at[rows_of(c)], r_send.at[c], r_recv.at[c], partner
-        )
-
-    def forcing_copy(c):
-        return remote(
-            forcing.at[rows_of(c), pl.ds(sent_at, sent_at)], forcing_far.at[rows_of(c)], f_send.at[c], f_recv.at[c], partner
-        )
-
-    def rim_copy(end, c):
+    def ratio_copy(u, span):
+        cells = pl.ds(sent_at, sent_at)
+        return remote(ratio.at[span, cells], ratio_far.at[span], send_sem.at[0], scale_recv.at[u], partner)
+
+    def forcing_copy(u, span):
+        cells = pl.ds(sent_at, sent_at)
+        return remote(forcing.at[span, cells], forcing_far.at[span], send_sem.at[1], scale_recv.at[u], partner)
+
+    def rim_copy(end, u, c):
         return remote(
             rim.at[end, rows_of(c)], field.at[0, (height, planes - 1)[end], pl.ds(1 + c * rows, rows), inner],
-            u_send.at[end, c], u_recv.at[end, c], partner,
+            send_sem.at[2], rim_recv.at[u], partner,
         )
 
     def back_copy(c):
         return remote(
             field.at[STEPS % 2, pl.ds(height, height), pl.ds(1 + c * rows, rows), inner], back.at[:, rows_of(c)],
-            b_send.at[c], b_recv.at[c], partner,
-        )
-
-    def xcopy(level, side, c):
+            send_sem.at[3], back_recv.at[c], partner,
+        )
+
+    def xcopy(level, side, u):
         return remote(
-            xsend.at[level, side, rows_of(c)], xrecv.at[level, 1 - side, rows_of(c)],
-            xsend_sem.at[level, side, c], xrecv_sem.at[level, 1 - side, c], beside("lon", (-1, 1)[side]),
+            xsend.at[level, u, side], xrecv.at[level, u, 1 - side],
+            send_sem.at[4], xrecv_sem.at[lax.rem(level, 2), u], beside("lon", (-1, 1)[side]),
         )
 
     def ycopy(level, side):
         p = lax.rem(level, 2)
         return remote(
             field.at[p, :, (1, depth)[side], inner], field.at[p, :, (depth + 1, 0)[side], inner],
-            ysend_sem.at[level, side], yrecv_sem.at[level, 1 - side], beside("lat", (-1, 1)[side]),
-        )
-
-    def core_xcopy(side, c):
+            ysend_sem.at[p], yrecv_sem.at[p], beside("lat", (-1, 1)[side]),
+        )
+
+    def core_xcopy(side, u):
         return remote(
-            csend.at[side, rows_of(c)], crecv.at[1 - side, rows_of(c)],
-            cxsend_sem.at[side, c], cxrecv_sem.at[1 - side, c], beside("lon", (-1, 1)[side]),
+            csend.at[u, side], crecv.at[u, 1 - side], send_sem.at[5], cxrecv_sem.at[u], beside("lon", (-1, 1)[side])
         )
 
     def core_ycopy(side):
         return remote(
             core.at[:, (1, depth)[side], inner], core.at[:, (depth + 1, 0)[side], inner],
-            cysend_sem.at[side], cyrecv_sem.at[1 - side], beside("lat", (-1, 1)[side]),
-        )
-
-    def stat_copy(offset, c):
+            send_sem.at[6], cyrecv_sem.at[0], beside("lat", (-1, 1)[side]),
+        )
+
+    def stat_copy(offset, i):
+        c = ordered(i)
         return remote(
-            stats.at[0, c], stats.at[offset, c], stat_send.at[offset - 1, c], stat_recv.at[offset - 1, c],
-            beside("lon", offset),
-        )
-
-    def at_ends(c, action):
-        for side, end in ((0, 0), (1, chunks - 1)):
-            @pl.when(c == end)
-            def _():
-                action(side)
+            stats.at[0, c], stats.at[offset, c], send_sem.at[7], stat_recv.at[lax.rem(i, 4)], beside("lon", offset)
+        )
+
+    def wait_all(ref, sem):
+        pltpu.make_async_copy(ref, ref, sem).wait()
 
     def over(count, body):
         def step(i, carry):
@@ -368,7 +364,7 @@
 
         over(rows, row)
 
-    def split_heat(slot, c):
+    def split_heat(u, slot, c):
         def row(i):
             y = c * rows + i
             for z in range(height):
@@ -382,9 +378,9 @@
                     else:
                         rim[min(z, 1), y, pl.ds(x, XBLOCK), :] = sent
             for side, x in ((0, PAD), (1, PAD + half - 1)):
-                csend[side, y] = jnp.zeros(csend.shape[2:], csend.dtype)
+                csend[u, side, slot * rows + i] = jnp.zeros(csend.shape[3:], csend.dtype)
                 for n in range(inside):
-                    csend[side, y, pl.ds(n, 1), :] = core[n, y + 1, pl.ds(x, 1), :]
+                    csend[u, side, slot * rows + i, pl.ds(n, 1), :] = core[n, y + 1, pl.ds(x, 1), :]
 
         over(rows, row)
 
@@ -397,14 +393,22 @@
         def _():
             pl.semaphore_wait(barrier, len(greeted))
 
-        ratio_copy(c).start()
+        ratio_copy(u, rows_of(c)).start()
         load(0, c, side).wait()
-        split_heat(side, c)
+        split_heat(u, side, c)
         for end in (0, 1):
-            rim_copy(end, c).start()
-        for end in (0, 1):
-            core_xcopy(end, c).start()
-        at_ends(c, lambda end: core_ycopy(end).start())
+            rim_copy(end, u, c).start()
+
+        @pl.when(side == 1)
+        def _():
+            for end in (0, 1):
+                core_xcopy(end, u).start()
+
+        @pl.when((side == 1) & (u == 0))
+        def _():
+            for end in (0, 1):
+                core_ycopy(end).start()
+
         load(2, c, side).wait()
         split_into(forcing, 2, side, c)
 
@@ -415,15 +419,21 @@
 
     def correct(u, side):
         c = chunk_of(u, side)
-        at_ends(c, lambda end: core_ycopy(1 - end).wait_recv())
-        for end in (0, 1):
-            core_xcopy(end, c).wait_recv()
+
+        @pl.when(side == 0)
+        def _():
+            wait_all(crecv.at[u], cxrecv_sem.at[u])
+
+        @pl.when((side == 0) & (u == 0))
+        def _():
+            wait_all(core.at[:, pl.ds(0, 2), inner], cyrecv_sem.at[0])
 
         def row(i):
             y = c * rows + i
-            mask = first_lanes(crecv.shape[2:])
-            left = turned(jnp.where(mask, csend[1, y], crecv[0, y]))
-            right = turned(jnp.where(mask, crecv[1, y], csend[0, y]))
+            k = side * rows + i
+            mask = first_lanes(crecv.shape[3:])
+            left = turned(jnp.where(mask, csend[u, 1, k], crecv[u, 0, k]))
+            right = turned(jnp.where(mask, crecv[u, 1, k], csend[u, 0, k]))
             for n in range(inside):
                 core[n, y + 1, pl.ds(PAD - 1, 1), :] = left[n:n + 1]
                 core[n, y + 1, pl.ds(PAD + half, 1), :] = right[n:n + 1]
@@ -443,7 +453,7 @@
                     forcing[y, cells, :] = forcing[y, cells, :] + ratio[y, cells, :] * sum(parts[1:], parts[0])
 
         over(rows, row)
-        forcing_copy(c).start()
+        forcing_copy(u, rows_of(c)).start()
 
     barrier = pltpu.get_barrier_semaphore()
     greeted = [partner, beside("lat", -1), beside("lat", 1)]
@@ -466,47 +476,63 @@
     over(units + 1, inputs)
 
 
-    def publish(level, c):
+    def publish(level, u):
         p = lax.rem(level, 2)
 
-        def row(i):
-            y = c * rows + i
+        def row(k):
+            y = chunk_of(u, k // rows) * rows + lax.rem(k, rows)
             for side, x in ((0, PAD), (1, PAD + half - 1)):
                 for z in range(planes):
-                    xsend[level, side, y, pl.ds(z, 1), :] = field[p, z, y + 1, pl.ds(x, 1), :]
-
-        over(rows, row)
+                    xsend[level, u, side, k, pl.ds(z, 1), :] = field[p, z, y + 1, pl.ds(x, 1), :]
+
+        over(2 * rows, row)
         for side in (0, 1):
-            xcopy(level, side, c).start()
-        at_ends(c, lambda side: ycopy(level, side).start())
-
-    def arrive(u, side):
-        c = chunk_of(u, side)
-        ratio_copy(c).wait_recv()
-        forcing_copy(c).wait_recv()
-        for end in (0, 1):
-            rim_copy(end, c).wait_recv()
-        publish(0, c)
-
-    def advance(s, u, side):
-        c = chunk_of(u, side)
+            xcopy(level, side, u).start()
+
+        @pl.when(u == 0)
+        def _():
+            for side in (0, 1):
+                ycopy(level, side).start()
+
+    def arrive(u):
+        wait_all(ratio_far.at[pl.ds(0, 4 * rows)], scale_recv.at[u])
+        wait_all(rim.at[:, pl.ds(0, 2 * rows)], rim_recv.at[u])
+        publish(0, u)
+
+    def advance(s, u):
         level = s - 1
         p = lax.rem(level, 2)
         q = 1 - p
-        at_ends(c, lambda end: ycopy(level, 1 - end).wait_recv())
-
-        @pl.when(s >= 2)
-        def _():
-            at_ends(c, lambda end: ycopy(s - 2, end).wait_send())
-
-        for end in (0, 1):
-            xcopy(level, end, c).wait_recv()
+
+        @pl.when(u == 0)
+        def _():
+            wait_all(field.at[p, :, pl.ds(0, 2), inner], yrecv_sem.at[p])
+
+        @pl.when((u == 0) & (s >= 2))
+        def _():
+            wait_all(field.at[q, :, pl.ds(0, 2), inner], ysend_sem.at[q])
+
+        wait_all(xrecv.at[level, u], xrecv_sem.at[p, u])
+        over(2, lambda side: march_rows(level, p, q, u, side))
+
+        @pl.when(s < STEPS)
+        def _():
+            publish(s, u)
+
+        @pl.when(s == STEPS)
+        def _():
+            for side in (0, 1):
+                back_copy(chunk_of(u, side)).start()
+
+    def march_rows(level, p, q, u, side):
+        c = chunk_of(u, side)
 
         def row(i):
             y = c * rows + i
-            mask = first_lanes(xrecv.shape[3:])
-            left = turned(jnp.where(mask, xsend[level, 1, y], xrecv[level, 0, y]))
-            right = turned(jnp.where(mask, xrecv[level, 1, y], xsend[level, 0, y]))
+            k = side * rows + i
+            mask = first_lanes(xrecv.shape[4:])
+            left = turned(jnp.where(mask, xsend[level, u, 1, k], xrecv[level, u, 0, k]))
+            right = turned(jnp.where(mask, xrecv[level, u, 1, k], xsend[level, u, 0, k]))
             for z in range(planes):
                 field[p, z, y + 1, pl.ds(PAD - 1, 1), :] = left[z:z + 1]
                 field[p, z, y + 1, pl.ds(PAD + half, 1), :] = right[z:z + 1]
@@ -532,34 +558,26 @@
 
         over(rows, row)
 
-        @pl.when(s < STEPS)
-        def _():
-            publish(s, c)
-
-        @pl.when(s == STEPS)
-        def _():
-            back_copy(c).start()
-
     def wave(w):
         @pl.when(w < units)
         def _():
-            over(2, lambda side: arrive(w, side))
+            arrive(w)
 
         def step(i):
             u = w - 1 - i
 
             @pl.when((u >= 0) & (u < units))
             def _():
-                over(2, lambda side: advance(i + 1, u, side))
+                advance(i + 1, u)
 
         over(STEPS, step)
 
     over(units + STEPS, wave)
 
 
-    def finish(c):
+    def finish(position):
+        c = ordered(position)
         back_copy(c).wait_recv()
-        forcing_copy(c).wait_send()
 
         def row(i):
             y = c * rows + i
@@ -585,11 +603,11 @@
 
         over(rows, row)
         for offset in range(1, counts["lon"]):
-            stat_copy(offset, c).start()
-
-    def combine(c):
-        for offset in range(1, counts["lon"]):
-            stat_copy(offset, c).wait_recv()
+            stat_copy(offset, position).start()
+
+    def combine(position):
+        c = ordered(position)
+        wait_all(stats.at[pl.ds(1, counts["lon"] - 1), c], stat_recv.at[lax.rem(position, 4)])
         means = [stats[offset, c, 0] for offset in range(counts["lon"])]
         mean = sum(means[1:], means[0]) * (1.0 / counts["lon"])
         squares = sum([stats[offset, c, 1] for offset in range(1, counts["lon"])], stats[0, c, 1])
@@ -597,42 +615,33 @@
         variance = (squares + width * apart) * (1.0 / (width * counts["lon"]))
         scale = lax.rsqrt(variance + 0.0001)
         for i in range(rows):
-            for copy in range(2):
-                for kind, values in ((0, mean), (1, scale)):
-                    moments_out[kind, c * rows + i, pl.ds(copy * height, height), :] = values[i * height:(i + 1) * height]
-        for offset in range(1, counts["lon"]):
-            stat_copy(offset, c).wait_send()
-
-    def ordered(i):
-        return chunk_of(i // 2, lax.rem(i, 2))
+            y = c * rows + i
+            lines = slice(i * height, (i + 1) * height)
+            pair_mean = jnp.concatenate([mean[lines]] * 2, axis=0)[None]
+            pair_scale = jnp.concatenate([scale[lines]] * 2, axis=0)[None]
+            values = heat_out[y]
+            tall = values.reshape(half, 2 * height, values.shape[1])
+            score_out[y] = ((tall - pair_mean) * pair_scale).reshape(values.shape)
+
+    wait_all(ratio.at[:, pl.ds(sent_at, sent_at)], send_sem.at[0])
+    wait_all(forcing.at[:, pl.ds(sent_at, sent_at)], send_sem.at[1])
 
     def ending(i):
-        finish(ordered(i))
+        finish(i)
 
         @pl.when(i > 0)
         def _():
-            combine(ordered(i - 1))
+            combine(i - 1)
 
     over(chunks, ending)
-
-    def drain(c):
-        ratio_copy(c).wait_send()
-        back_copy(c).wait_send()
-        for side in (0, 1):
-            rim_copy(side, c).wait_send()
-            core_xcopy(side, c).wait_send()
-
-        def level_sent(level):
-            for side in (0, 1):
-                xcopy(level, side, c).wait_send()
-
-        over(STEPS, level_sent)
-
-    over(chunks, drain)
-    for side in (0, 1):
-        core_ycopy(side).wait_send()
-        ycopy(STEPS - 1, side).wait_send()
-    combine(ordered(chunks - 1))
+    wait_all(rim, send_sem.at[2])
+    wait_all(field.at[STEPS % 2, pl.ds(height, height), pl.ds(1, depth), inner], send_sem.at[3])
+    wait_all(xsend, send_sem.at[4])
+    wait_all(csend, send_sem.at[5])
+    wait_all(core.at[:, pl.ds(0, 2), inner], send_sem.at[6])
+    wait_all(field.at[(STEPS - 1) % 2, :, pl.ds(0, 2), inner], ysend_sem.at[(STEPS - 1) % 2])
+    wait_all(stats.at[pl.ds(1, counts["lon"] - 1)], send_sem.at[7])
+    combine(chunks - 1)
 
 
 def swap(sizes, arrays):
@@ -640,6 +649,7 @@
     members = arrays[0].shape[-1]
     rows = 2
     chunks = depth // rows
+    units = chunks // 2
     half = width // 2
     lon = lax.axis_size("lon")
     flat = (depth, width * height, members)
@@ -648,34 +658,26 @@
     vmem = lambda *shape: pltpu.VMEM((*shape, members), f32)
     return pl.pallas_call(
         functools.partial(swap_kernel, sizes, rows),
-        out_shape=(pltpu.VMEM(flat, f32), pltpu.VMEM((2, depth, 2 * height, members), f32)),
+        out_shape=(pltpu.VMEM(flat, f32),) * 2,
         in_specs=[pl.BlockSpec(memory_space=pl.ANY)] * 3,
         out_specs=(pl.BlockSpec(memory_space=pltpu.VMEM),) * 2,
         scratch_shapes=[
             vmem(2, 2 * height, depth + 2, half + 2 * PAD),
             vmem(2, depth, half),
             vmem(height - 2, depth + 2, half + 2 * PAD),
-            vmem(depth, width * height),
             vmem(depth, half * height),
             vmem(depth, half * height),
             vmem(height, depth, half),
             vmem(3, 2, rows, width * height),
-            vmem(STEPS, 2, depth, 2 * height), vmem(STEPS, 2, depth, 2 * height),
-            vmem(2, depth, 8), vmem(2, depth, 8),
+            vmem(STEPS, units, 2, 2 * rows, 2 * height), vmem(STEPS, units, 2, 2 * rows, 2 * height),
+            vmem(units, 2, 2 * rows, 8), vmem(units, 2, 2 * rows, 8),
             vmem(lon, chunks, 2, rows * height),
-            dma((3, 2)),
-            dma((chunks,)), dma((chunks,)),
-            dma((2, chunks)), dma((2, chunks)),
-            dma((chunks,)), dma((chunks,)),
-            dma((chunks,)), dma((chunks,)),
-            dma((STEPS, 2, chunks)), dma((STEPS, 2, chunks)),
-            dma((STEPS, 2)), dma((STEPS, 2)),
-            dma((2, chunks)), dma((2, chunks)),
-            dma((2,)), dma((2,)),
-            dma((lon - 1, chunks)), dma((lon - 1, chunks)),
+            dma((3, 2)), dma((8,)), dma((2,)),
+            dma((units,)), dma((units,)), dma((chunks,)),
+            dma((2, units)), dma((2,)), dma((units,)), dma((1,)), dma((4,)),
         ],
         compiler_params=pltpu.CompilerParams(
-            collective_id=1, has_side_effects=True, vmem_limit_bytes=54 * 1024 * 1024
+            collective_id=1, has_side_effects=True, vmem_limit_bytes=47 * 1024 * 1024
         ),
         name="swap",
     )(*arrays)
@@ -716,6 +718,19 @@
     )(*arrays)
 
 
+def copy_kernel(chunks, heat, scored, score, end, sem):
+    rows = heat.shape[0] // chunks
+    copies = []
+    for c in range(chunks):
+        span = pl.ds(c * rows, rows)
+        copies.append(pltpu.make_async_copy(heat.at[span], end.at[span], sem.at[0, c]))
+        copies.append(pltpu.make_async_copy(scored.at[span], score.at[span], sem.at[1, c]))
+    for copy in copies:
+        copy.start()
+    for copy in copies:
+        copy.wait()
+
+
 def score_kernel(chunks, heat, moments, score, end, scaled, score_sem, end_sem):
     rows = heat.shape[0] // chunks
     finish = pltpu.make_async_copy(heat, end, end_sem)
@@ -756,17 +771,25 @@
     arrays = [a.reshape(flat) for a in (initial_heat, diffusivity_ratio, forcing_term)]
     swaps = lax.axis_size("lev") == 2 and 3 <= height and 3 * height + 2 < 4 * STEPS
     swaps = swaps and depth % 4 == 0 and width % (2 * XBLOCK) == 0
-    heat, moments = (swap if swaps else march)((depth, width, height), arrays)
-    parts = min(8, depth)
-    score, end = pl.pallas_call(
-        functools.partial(score_kernel, parts),
-        out_shape=(jax.ShapeDtypeStruct(flat, f32),) * 2,
-        in_specs=[pl.BlockSpec(memory_space=pltpu.VMEM)] * 2,
-        out_specs=(anywhere,) * 2,
-        scratch_shapes=[pltpu.VMEM(flat, f32), dma((parts,)), dma(())],
-        compiler_params=pltpu.CompilerParams(vmem_limit_bytes=24 * 1024 * 1024),
-        name="score",
-    )(heat, moments)
+    sizes = (depth, width, height)
+    common = dict(out_shape=(jax.ShapeDtypeStruct(flat, f32),) * 2, out_specs=(anywhere,) * 2)
+    inputs = [pl.BlockSpec(memory_space=pltpu.VMEM)] * 2
+    if swaps:
+        parts = min(4, depth)
+        score, end = pl.pallas_call(
+            functools.partial(copy_kernel, parts), **common, in_specs=inputs,
+            scratch_shapes=[dma((2, parts))],
+            compiler_params=pltpu.CompilerParams(vmem_limit_bytes=8 * 1024 * 1024),
+            name="emit",
+        )(*swap(sizes, arrays))
+    else:
+        parts = min(8, depth)
+        score, end = pl.pallas_call(
+            functools.partial(score_kernel, parts), **common, in_specs=inputs,
+            scratch_shapes=[pltpu.VMEM(flat, f32), dma((parts,)), dma(())],
+            compiler_params=pltpu.CompilerParams(vmem_limit_bytes=24 * 1024 * 1024),
+            name="score",
+        )(*march(sizes, arrays))
     return score.reshape(initial_heat.shape), end.reshape(initial_heat.shape)
 
 

time: 338 us -> 333 us (0.985)
  Pallas kernels: 337 us -> 332 us
    pallas_call x1, Pallas kernels: 331 us -> 326 us  [swap(): pl.pallas_call(functools.partial(swap_kernel, sizes, rows), out_shape=(pl...]
where the time goes in v2:
time: 333 us
  Pallas kernels  332 us (100%)
    pallas_call x1, Pallas kernels, swap(): pl.pallas_call(functools.partial(swap_kernel, sizes, rows), out_shape=(pl...  326 us

profile of v2, /device:TPU:0, one launch (start us, length us, event | category | flops | bytes accessed | tf_op | source)
XLA Modules:
  0.0 333.0 jit_solution(13452634857603619089)
XLA Ops:
  0.6 326.5 %swap.1 = (f32[32,512,128]{2,1,0:T(8,128)S(1)}, f32[32,512,128]{2,1,0:T(8,128)S(1)}) custom-call(f32[32,512,128]{2,1,0:T(8,128)} %bitcast.5, f32[32,512,128]{2,1,0:T(8,128)} %bitcast.6, f32[32,512,128]{2,1,0:T(8,128)} %bitcast.7), custom_call_target="tpu_custom_call" | custom-call | tf_op jit(solution)/shard_map/swap/pallas_call | solution.py:659
  327.1 5.9 %emit.1 = (f32[32,512,128]{2,1,0:T(8,128)}, f32[32,512,128]{2,1,0:T(8,128)}) custom-call(f32[32,512,128]{2,1,0:T(8,128)S(1)} %get-tuple-element.6.heat, f32[32,512,128]{2,1,0:T(8,128)S(1)} %get-tuple-element.7.scored), custom_call_target="tpu_custom_call" | custom-call | tf_op jit(solution)/shard_map/emit/pallas_call | solution.py:779

commit v3 on v2

--- a/solution.py
+++ b/solution.py
@@ -240,8 +240,8 @@
     sizes, rows,
     heat_in, ratio_in, forcing_in, heat_out, score_out,
     field, rim, core, ratio_far, forcing_far, back, stage,
-    xsend, xrecv, csend, crecv, stats,
-    load_sem, send_sem, ysend_sem, scale_recv, rim_recv, back_recv,
+    xsend, xrecv, csend, crecv, ends, ends_far, stats, moments,
+    load_sem, send_sem, ysend_sem, scale_recv, rim_recv, inner_recv, ends_recv, outer_recv,
     xrecv_sem, yrecv_sem, cxrecv_sem, cyrecv_sem, stat_recv,
 ):
     depth, width, height = sizes
@@ -267,9 +267,6 @@
     def first_lanes(shape):
         return lax.broadcasted_iota(jnp.int32, shape, 1) < shape[1] // 2
 
-    def ordered(i):
-        return chunk_of(i // 2, lax.rem(i, 2))
-
     def turned(values):
         return pltpu.roll(values, values.shape[1] // 2, 1)
 
@@ -299,11 +296,20 @@
             send_sem.at[2], rim_recv.at[u], partner,
         )
 
-    def back_copy(c):
+    def inner_copy(u, c):
         return remote(
-            field.at[STEPS % 2, pl.ds(height, height), pl.ds(1 + c * rows, rows), inner], back.at[:, rows_of(c)],
-            send_sem.at[3], back_recv.at[c], partner,
-        )
+            field.at[STEPS % 2, pl.ds(height + 1, inside), pl.ds(1 + c * rows, rows), inner],
+            back.at[pl.ds(1, inside), rows_of(c)], send_sem.at[3], inner_recv.at[u], partner,
+        )
+
+    def outer_copy(end, u, c):
+        return remote(
+            field.at[STEPS % 2, (height, planes - 1)[end], pl.ds(1 + c * rows, rows), inner],
+            back.at[(0, height - 1)[end], rows_of(c)], send_sem.at[3], outer_recv.at[u], partner,
+        )
+
+    def ends_copy(u):
+        return remote(ends.at[1, u], ends_far.at[u], send_sem.at[8], ends_recv.at[u], partner)
 
     def xcopy(level, side, u):
         return remote(
@@ -329,10 +335,9 @@
             send_sem.at[6], cyrecv_sem.at[0], beside("lat", (-1, 1)[side]),
         )
 
-    def stat_copy(offset, i):
-        c = ordered(i)
+    def stat_copy(offset, u):
         return remote(
-            stats.at[0, c], stats.at[offset, c], send_sem.at[7], stat_recv.at[lax.rem(i, 4)], beside("lon", offset)
+            stats.at[0, u], stats.at[offset, u], send_sem.at[7], stat_recv.at[lax.rem(u, 2)], beside("lon", offset)
         )
 
     def wait_all(ref, sem):
@@ -480,7 +485,7 @@
         p = lax.rem(level, 2)
 
         def row(k):
-            y = chunk_of(u, k // rows) * rows + lax.rem(k, rows)
+            y = row_of(u, k)
             for side, x in ((0, PAD), (1, PAD + half - 1)):
                 for z in range(planes):
                     xsend[level, u, side, k, pl.ds(z, 1), :] = field[p, z, y + 1, pl.ds(x, 1), :]
@@ -522,7 +527,29 @@
         @pl.when(s == STEPS)
         def _():
             for side in (0, 1):
-                back_copy(chunk_of(u, side)).start()
+                inner_copy(u, chunk_of(u, side)).start()
+            over(2 * rows, lambda k: end_moments(u, k))
+            ends_copy(u).start()
+            for side in (0, 1):
+                for end in (0, 1):
+                    outer_copy(end, u, chunk_of(u, side)).start()
+
+    def row_of(u, k):
+        return chunk_of(u, k // rows) * rows + lax.rem(k, rows)
+
+    def end_moments(u, k):
+        for whose in (0, 1):
+            for end in (0, 1):
+                line = field[STEPS % 2, whose * height + end * (height - 1), row_of(u, k) + 1, inner, :]
+                mean = both_halves(jnp.sum(line, axis=0, keepdims=True)) * (1.0 / width)
+                centred = line - mean
+                ends[whose, u, 0, pl.ds(2 * k + end, 1), :] = mean
+                squares = both_halves(jnp.sum(centred * centred, axis=0, keepdims=True))
+                ends[whose, u, 1, pl.ds(2 * k + end, 1), :] = squares
+
+    def both_halves(sums):
+        tall = jnp.broadcast_to(sums, (8, sums.shape[1]))
+        return (tall + turned(tall))[:1]
 
     def march_rows(level, p, q, u, side):
         c = chunk_of(u, side)
@@ -575,65 +602,75 @@
     over(units + STEPS, wave)
 
 
-    def finish(position):
-        c = ordered(position)
-        back_copy(c).wait_recv()
-
-        def row(i):
-            y = c * rows + i
-            for z in range(height):
-                parts = []
-                for x in range(0, half, XBLOCK):
-                    here = pl.ds(PAD + x, XBLOCK)
-                    kept, other = field[STEPS % 2, z, y + 1, here, :], back[z, y, pl.ds(x, XBLOCK), :]
-                    if 0 < z < height - 1:
-                        other = other + core[z - 1, y + 1, here, :]
-                    mask = first_lanes(kept.shape)
-                    one, two = jnp.where(upper, other, kept), jnp.where(upper, kept, other)
-                    low = jnp.where(mask, one, turned(two))
-                    high = jnp.where(mask, turned(one), two)
-                    heat_out[y, pl.ds(x * height + z, XBLOCK, stride=height), :] = low
-                    heat_out[y, pl.ds((half + x) * height + z, XBLOCK, stride=height), :] = high
-                    parts += [low, high]
-                line = jnp.concatenate(parts, axis=0)
-                mean = jnp.sum(line, axis=0, keepdims=True) * (1.0 / width)
-                centred = line - mean
-                stats[0, c, 0, pl.ds(i * height + z, 1), :] = mean
-                stats[0, c, 1, pl.ds(i * height + z, 1), :] = jnp.sum(centred * centred, axis=0, keepdims=True)
-
-        over(rows, row)
+    def join(y, z, x):
+        here = pl.ds(PAD + x, XBLOCK)
+        kept, other = field[STEPS % 2, z, y + 1, here, :], back[z, y, pl.ds(x, XBLOCK), :]
+        if 0 < z < height - 1:
+            other = other + core[z - 1, y + 1, here, :]
+        mask = first_lanes(kept.shape)
+        one, two = jnp.where(upper, other, kept), jnp.where(upper, kept, other)
+        low = jnp.where(mask, one, turned(two))
+        high = jnp.where(mask, turned(one), two)
+        heat_out[y, pl.ds(x * height + z, XBLOCK, stride=height), :] = low
+        heat_out[y, pl.ds((half + x) * height + z, XBLOCK, stride=height), :] = high
+        return [low, high]
+
+    def join_inner(u, k):
+        y = row_of(u, k)
+        for z in range(1, height - 1):
+            line = jnp.concatenate(sum([join(y, z, x) for x in range(0, half, XBLOCK)], []), axis=0)
+            mean = jnp.sum(line, axis=0, keepdims=True) * (1.0 / width)
+            centred = line - mean
+            stats[0, u, 0, pl.ds(k * height + z, 1), :] = mean
+            stats[0, u, 1, pl.ds(k * height + z, 1), :] = jnp.sum(centred * centred, axis=0, keepdims=True)
+
+    def share_moments(u):
+        mask = first_lanes(ends_far.shape[2:])
+        for kind in (0, 1):
+            mine, far = ends[0, u, kind], ends_far[u, kind]
+            lines = jnp.where(upper, jnp.where(mask, far, mine), jnp.where(mask, mine, far))
+            for k in range(2 * rows):
+                for end in (0, 1):
+                    at = k * height + end * (height - 1)
+                    stats[0, u, kind, pl.ds(at, 1), :] = lines[2 * k + end:2 * k + end + 1]
         for offset in range(1, counts["lon"]):
-            stat_copy(offset, position).start()
-
-    def combine(position):
-        c = ordered(position)
-        wait_all(stats.at[pl.ds(1, counts["lon"] - 1), c], stat_recv.at[lax.rem(position, 4)])
-        means = [stats[offset, c, 0] for offset in range(counts["lon"])]
+            stat_copy(offset, u).start()
+
+    def combine(u):
+        wait_all(stats.at[pl.ds(1, counts["lon"] - 1), u], stat_recv.at[lax.rem(u, 2)])
+        means = [stats[offset, u, 0] for offset in range(counts["lon"])]
         mean = sum(means[1:], means[0]) * (1.0 / counts["lon"])
-        squares = sum([stats[offset, c, 1] for offset in range(1, counts["lon"])], stats[0, c, 1])
+        squares = sum([stats[offset, u, 1] for offset in range(1, counts["lon"])], stats[0, u, 1])
         apart = sum([(other - mean) * (other - mean) for other in means[1:]], (means[0] - mean) * (means[0] - mean))
         variance = (squares + width * apart) * (1.0 / (width * counts["lon"]))
         scale = lax.rsqrt(variance + 0.0001)
-        for i in range(rows):
-            y = c * rows + i
-            lines = slice(i * height, (i + 1) * height)
-            pair_mean = jnp.concatenate([mean[lines]] * 2, axis=0)[None]
-            pair_scale = jnp.concatenate([scale[lines]] * 2, axis=0)[None]
-            values = heat_out[y]
-            tall = values.reshape(half, 2 * height, values.shape[1])
-            score_out[y] = ((tall - pair_mean) * pair_scale).reshape(values.shape)
+        for k in range(2 * rows):
+            for copy in range(2):
+                for kind, values in ((0, mean), (1, scale)):
+                    moments[kind, k, pl.ds(copy * height, height), :] = values[k * height:(k + 1) * height]
+
+    def join_outer(u, k):
+        y = row_of(u, k)
+        for z in (0, height - 1):
+            for x in range(0, half, XBLOCK):
+                join(y, z, x)
+        values = heat_out[y]
+        tall = values.reshape(half, 2 * height, values.shape[1])
+        score_out[y] = ((tall - moments[0, k][None]) * moments[1, k][None]).reshape(values.shape)
 
     wait_all(ratio.at[:, pl.ds(sent_at, sent_at)], send_sem.at[0])
     wait_all(forcing.at[:, pl.ds(sent_at, sent_at)], send_sem.at[1])
 
-    def ending(i):
-        finish(i)
-
-        @pl.when(i > 0)
-        def _():
-            combine(i - 1)
-
-    over(chunks, ending)
+    def finish(u):
+        wait_all(back.at[pl.ds(0, inside), pl.ds(0, 2 * rows)], inner_recv.at[u])
+        over(2 * rows, lambda k: join_inner(u, k))
+        wait_all(ends_far.at[u], ends_recv.at[u])
+        share_moments(u)
+        combine(u)
+        wait_all(back.at[pl.ds(0, 2), pl.ds(0, 2 * rows)], outer_recv.at[u])
+        over(2 * rows, lambda k: join_outer(u, k))
+
+    over(units, finish)
     wait_all(rim, send_sem.at[2])
     wait_all(field.at[STEPS % 2, pl.ds(height, height), pl.ds(1, depth), inner], send_sem.at[3])
     wait_all(xsend, send_sem.at[4])
@@ -641,7 +678,7 @@
     wait_all(core.at[:, pl.ds(0, 2), inner], send_sem.at[6])
     wait_all(field.at[(STEPS - 1) % 2, :, pl.ds(0, 2), inner], ysend_sem.at[(STEPS - 1) % 2])
     wait_all(stats.at[pl.ds(1, counts["lon"] - 1)], send_sem.at[7])
-    combine(chunks - 1)
+    wait_all(ends_far, send_sem.at[8])
 
 
 def swap(sizes, arrays):
@@ -671,10 +708,11 @@
             vmem(3, 2, rows, width * height),
             vmem(STEPS, units, 2, 2 * rows, 2 * height), vmem(STEPS, units, 2, 2 * rows, 2 * height),
             vmem(units, 2, 2 * rows, 8), vmem(units, 2, 2 * rows, 8),
-            vmem(lon, chunks, 2, rows * height),
-            dma((3, 2)), dma((8,)), dma((2,)),
-            dma((units,)), dma((units,)), dma((chunks,)),
-            dma((2, units)), dma((2,)), dma((units,)), dma((1,)), dma((4,)),
+            vmem(2, units, 2, 4 * rows), vmem(units, 2, 4 * rows),
+            vmem(lon, units, 2, 2 * rows * height), vmem(2, 2 * rows, 2 * height),
+            dma((3, 2)), dma((9,)), dma((2,)),
+            dma((units,)), dma((units,)), dma((units,)), dma((units,)), dma((units,)),
+            dma((2, units)), dma((2,)), dma((units,)), dma((1,)), dma((2,)),
         ],
         compiler_params=pltpu.CompilerParams(
             collective_id=1, has_side_effects=True, vmem_limit_bytes=47 * 1024 * 1024

time: 333 us -> 331 us (level)
  no operation moved by 1% of the time
where the time goes in v3:
time: 331 us
  Pallas kernels  330 us (100%)
    pallas_call x1, Pallas kernels, swap(): pl.pallas_call(functools.partial(swap_kernel, sizes, rows), out_shape=(pl...  324 us

profile of v3, /device:TPU:0, one launch (start us, length us, event | category | flops | bytes accessed | tf_op | source)
XLA Modules:
  0.0 330.9 jit_solution(5892454958551005578)
XLA Ops:
  0.6 324.4 %swap.1 = (f32[32,512,128]{2,1,0:T(8,128)S(1)}, f32[32,512,128]{2,1,0:T(8,128)S(1)}) custom-call(f32[32,512,128]{2,1,0:T(8,128)} %bitcast.5, f32[32,512,128]{2,1,0:T(8,128)} %bitcast.6, f32[32,512,128]{2,1,0:T(8,128)} %bitcast.7), custom_call_target="tpu_custom_call" | custom-call | tf_op jit(solution)/shard_map/swap/pallas_call | solution.py:696
  325.0 5.9 %emit.1 = (f32[32,512,128]{2,1,0:T(8,128)}, f32[32,512,128]{2,1,0:T(8,128)}) custom-call(f32[32,512,128]{2,1,0:T(8,128)S(1)} %get-tuple-element.6.heat, f32[32,512,128]{2,1,0:T(8,128)S(1)} %get-tuple-element.7.scored), custom_call_target="tpu_custom_call" | custom-call | tf_op jit(solution)/shard_map/emit/pallas_call | solution.py:817

commit v4 on v3

--- a/solution.py
+++ b/solution.py
@@ -238,11 +238,11 @@
 
 def swap_kernel(
     sizes, rows,
-    heat_in, ratio_in, forcing_in, heat_out, score_out,
+    heat_in, ratio_in, forcing_in, heat_out, score_out, seam_far, seam_near, seam_rows, moments,
     field, rim, core, ratio_far, forcing_far, back, stage,
-    xsend, xrecv, csend, crecv, ends, ends_far, stats, moments,
+    xsend, xrecv, csend, crecv, ends, ends_far, stats,
     load_sem, send_sem, ysend_sem, scale_recv, rim_recv, inner_recv, ends_recv, outer_recv,
-    xrecv_sem, yrecv_sem, cxrecv_sem, cyrecv_sem, stat_recv,
+    xrecv_sem, yrecv_sem, cxrecv_sem, cyrecv_sem, stat_recv, seam_sem,
 ):
     depth, width, height = sizes
     half, planes, inside = width // 2, 2 * height, height - 2
@@ -305,7 +305,7 @@
     def outer_copy(end, u, c):
         return remote(
             field.at[STEPS % 2, (height, planes - 1)[end], pl.ds(1 + c * rows, rows), inner],
-            back.at[(0, height - 1)[end], rows_of(c)], send_sem.at[3], outer_recv.at[u], partner,
+            back.at[(0, height - 1)[end], rows_of(c)], send_sem.at[9], outer_recv.at[u], partner,
         )
 
     def ends_copy(u):
@@ -530,9 +530,27 @@
                 inner_copy(u, chunk_of(u, side)).start()
             over(2 * rows, lambda k: end_moments(u, k))
             ends_copy(u).start()
+
+        @pl.when((s == STEPS) & (u > 0))
+        def _():
             for side in (0, 1):
                 for end in (0, 1):
-                    outer_copy(end, u, chunk_of(u, side)).start()
+                    outer_copy(end, u - 1, chunk_of(u - 1, side)).start()
+
+        @pl.when((s == STEPS) & (u == units - 1))
+        def _():
+            over(2 * rows, lambda k: keep_seam(u, k))
+            for end in (0, 1):
+                seam_copy(end).start()
+
+    def keep_seam(u, k):
+        for end in (0, 1):
+            seam_near[end, k] = field[STEPS % 2, end * (height - 1), row_of(u, k) + 1, inner, :]
+
+    def seam_copy(end):
+        span = pl.ds((units - 1) * rows + 1, 2 * rows)
+        plane = field.at[STEPS % 2, (height, planes - 1)[end], span, inner]
+        return pltpu.make_async_copy(plane, seam_far.at[end], seam_sem.at[end])
 
     def row_of(u, k):
         return chunk_of(u, k // rows) * rows + lax.rem(k, rows)
@@ -647,7 +665,7 @@
         for k in range(2 * rows):
             for copy in range(2):
                 for kind, values in ((0, mean), (1, scale)):
-                    moments[kind, k, pl.ds(copy * height, height), :] = values[k * height:(k + 1) * height]
+                    moments[u, kind, k, pl.ds(copy * height, height), :] = values[k * height:(k + 1) * height]
 
     def join_outer(u, k):
         y = row_of(u, k)
@@ -656,7 +674,7 @@
                 join(y, z, x)
         values = heat_out[y]
         tall = values.reshape(half, 2 * height, values.shape[1])
-        score_out[y] = ((tall - moments[0, k][None]) * moments[1, k][None]).reshape(values.shape)
+        score_out[y] = ((tall - moments[u, 0, k][None]) * moments[u, 1, k][None]).reshape(values.shape)
 
     wait_all(ratio.at[:, pl.ds(sent_at, sent_at)], send_sem.at[0])
     wait_all(forcing.at[:, pl.ds(sent_at, sent_at)], send_sem.at[1])
@@ -667,12 +685,23 @@
         wait_all(ends_far.at[u], ends_recv.at[u])
         share_moments(u)
         combine(u)
-        wait_all(back.at[pl.ds(0, 2), pl.ds(0, 2 * rows)], outer_recv.at[u])
-        over(2 * rows, lambda k: join_outer(u, k))
+
+        @pl.when(u > 0)
+        def _():
+            wait_all(back.at[pl.ds(0, 2), pl.ds(0, 2 * rows)], outer_recv.at[u - 1])
+            over(2 * rows, lambda k: join_outer(u - 1, k))
 
     over(units, finish)
+
+    def seam_row(k):
+        seam_rows[k] = heat_out[row_of(units - 1, k)]
+
+    over(2 * rows, seam_row)
     wait_all(rim, send_sem.at[2])
-    wait_all(field.at[STEPS % 2, pl.ds(height, height), pl.ds(1, depth), inner], send_sem.at[3])
+    for end in (0, 1):
+        seam_copy(end).wait()
+    wait_all(field.at[STEPS % 2, pl.ds(height + 1, inside), pl.ds(1, depth), inner], send_sem.at[3])
+    wait_all(field.at[STEPS % 2, pl.ds(height, 2), pl.ds(1, depth - 2 * rows), inner], send_sem.at[9])
     wait_all(xsend, send_sem.at[4])
     wait_all(csend, send_sem.at[5])
     wait_all(core.at[:, pl.ds(0, 2), inner], send_sem.at[6])
@@ -695,9 +724,13 @@
     vmem = lambda *shape: pltpu.VMEM((*shape, members), f32)
     return pl.pallas_call(
         functools.partial(swap_kernel, sizes, rows),
-        out_shape=(pltpu.VMEM(flat, f32),) * 2,
+        out_shape=(
+            pltpu.VMEM(flat, f32), pltpu.VMEM(flat, f32),
+            jax.ShapeDtypeStruct((2, 2 * rows, half, members), f32), vmem(2, 2 * rows, half),
+            vmem(2 * rows, width * height), vmem(units, 2, 2 * rows, 2 * height),
+        ),
         in_specs=[pl.BlockSpec(memory_space=pl.ANY)] * 3,
-        out_specs=(pl.BlockSpec(memory_space=pltpu.VMEM),) * 2,
+        out_specs=tuple(pl.BlockSpec(memory_space=pltpu.HBM if i == 2 else pltpu.VMEM) for i in range(6)),
         scratch_shapes=[
             vmem(2, 2 * height, depth + 2, half + 2 * PAD),
             vmem(2, depth, half),
@@ -709,13 +742,13 @@
             vmem(STEPS, units, 2, 2 * rows, 2 * height), vmem(STEPS, units, 2, 2 * rows, 2 * height),
             vmem(units, 2, 2 * rows, 8), vmem(units, 2, 2 * rows, 8),
             vmem(2, units, 2, 4 * rows), vmem(units, 2, 4 * rows),
-            vmem(lon, units, 2, 2 * rows * height), vmem(2, 2 * rows, 2 * height),
-            dma((3, 2)), dma((9,)), dma((2,)),
+            vmem(lon, units, 2, 2 * rows * height),
+            dma((3, 2)), dma((10,)), dma((2,)),
             dma((units,)), dma((units,)), dma((units,)), dma((units,)), dma((units,)),
-            dma((2, units)), dma((2,)), dma((units,)), dma((1,)), dma((2,)),
+            dma((2, units)), dma((2,)), dma((units,)), dma((1,)), dma((2,)), dma((2,)),
         ],
         compiler_params=pltpu.CompilerParams(
-            collective_id=1, has_side_effects=True, vmem_limit_bytes=47 * 1024 * 1024
+            collective_id=1, has_side_effects=True, vmem_limit_bytes=46 * 1024 * 1024
         ),
         name="swap",
     )(*arrays)
@@ -769,6 +802,43 @@
         copy.wait()
 
 
+def seam_kernel(sizes, far, near, rows_in, moments, score_in, end_in, score, end, joined, scored, sem):
+    width, height, first = sizes
+    half = width // 2
+    unit = moments.shape[0] - 1
+    upper = lax.axis_index("lev") == 1
+
+    def out_copies(k):
+        return [
+            pltpu.make_async_copy(source.at[k], target.at[first + k], sem.at[kind, k])
+            for kind, (source, target) in enumerate(((joined, end), (scored, score)))
+        ]
+
+    def row(k, carry):
+        joined[k] = rows_in[k]
+        for side, z in ((0, 0), (1, height - 1)):
+            for x in range(0, half, XBLOCK):
+                kept, other = near[side, k, pl.ds(x, XBLOCK), :], far[side, k, pl.ds(x, XBLOCK), :]
+                mask = lax.broadcasted_iota(jnp.int32, kept.shape, 1) < kept.shape[1] // 2
+                one, two = jnp.where(upper, other, kept), jnp.where(upper, kept, other)
+                turn = kept.shape[1] // 2
+                joined[k, pl.ds(x * height + z, XBLOCK, stride=height), :] = jnp.where(mask, one, pltpu.roll(two, turn, 1))
+                joined[k, pl.ds((half + x) * height + z, XBLOCK, stride=height), :] = jnp.where(
+                    mask, pltpu.roll(one, turn, 1), two
+                )
+        out_copies(k)[0].start()
+        values = joined[k]
+        tall = values.reshape(half, 2 * height, values.shape[1])
+        scored[k] = ((tall - moments[unit, 0, k][None]) * moments[unit, 1, k][None]).reshape(values.shape)
+        out_copies(k)[1].start()
+        return carry
+
+    lax.fori_loop(0, joined.shape[0], row, 0)
+    for k in range(joined.shape[0]):
+        for copy in out_copies(k):
+            copy.wait()
+
+
 def score_kernel(chunks, heat, moments, score, end, scaled, score_sem, end_sem):
     rows = heat.shape[0] // chunks
     finish = pltpu.make_async_copy(heat, end, end_sem)
@@ -813,13 +883,27 @@
     common = dict(out_shape=(jax.ShapeDtypeStruct(flat, f32),) * 2, out_specs=(anywhere,) * 2)
     inputs = [pl.BlockSpec(memory_space=pltpu.VMEM)] * 2
     if swaps:
+        heat, scored, far, near, seam_rows, moments = swap(sizes, arrays)
+        far = lax.ppermute(far, "lev", [(0, 1), (1, 0)])
         parts = min(4, depth)
+        in_hbm = pl.BlockSpec(memory_space=pltpu.HBM)
         score, end = pl.pallas_call(
-            functools.partial(copy_kernel, parts), **common, in_specs=inputs,
-            scratch_shapes=[dma((2, parts))],
+            functools.partial(copy_kernel, parts), out_shape=common["out_shape"], out_specs=(in_hbm,) * 2,
+            in_specs=inputs, scratch_shapes=[dma((2, parts))],
+            cost_estimate=pl.CostEstimate(flops=60000000, bytes_accessed=4 * heat.nbytes, transcendentals=0),
             compiler_params=pltpu.CompilerParams(vmem_limit_bytes=8 * 1024 * 1024),
             name="emit",
-        )(*swap(sizes, arrays))
+        )(heat, scored)
+        taken = seam_rows.shape[0]
+        score, end = pl.pallas_call(
+            functools.partial(seam_kernel, (width, height, (depth - taken) // 2)),
+            out_shape=common["out_shape"], out_specs=(in_hbm,) * 2,
+            in_specs=[pl.BlockSpec(memory_space=pltpu.VMEM)] * 4 + [in_hbm] * 2,
+            scratch_shapes=[pltpu.VMEM(seam_rows.shape, f32)] * 2 + [dma((2, taken))],
+            input_output_aliases={4: 0, 5: 1},
+            compiler_params=pltpu.CompilerParams(vmem_limit_bytes=8 * 1024 * 1024),
+            name="seam",
+        )(far, near, seam_rows, moments, score, end)
     else:
         parts = min(8, depth)
         score, end = pl.pallas_call(

time: 331 us -> 329 us (level)
  Pallas kernels: 330 us -> 326 us
    pallas_call x1, Pallas kernels: 324 us -> 319 us  [swap(): pl.pallas_call(functools.partial(swap_kernel, sizes, rows), out_shape=(pl...]
    pallas_call x1 -> x2, Pallas kernels: 5.92 us -> 7.4 us  [the longest x1 5.92 us: local(): pl.pallas_call(functools.partial(copy_kernel, parts), out_shape=common['o...]
  transfers between devices with their start and end apart: 0 -> 1, of which waited for: 0 -> 1; matrix products, arithmetic and copies ran while one was open for 0% -> 0% of each run, Pallas kernels for 0% -> 2%
where the time goes in v4:
time: 329 us; the launch traced here: 328 us
  Pallas kernels  326 us (99%)
    pallas_call x1, Pallas kernels, swap(): pl.pallas_call(functools.partial(swap_kernel, sizes, rows), out_shape=(pl...  319 us
  transfers between devices with their start and end apart: 1, of which 1 were waited for; matrix products, arithmetic and copies ran while one was open for 0% of the time, Pallas kernels for 2%

profile of v4, /device:TPU:0, one launch (start us, length us, event | category | flops | bytes accessed | tf_op | source)
XLA Modules:
  0.0 328.5 jit_solution(10575028488982202795)
XLA Ops:
  0.6 318.9 %swap.1 = (f32[32,512,128]{2,1,0:T(8,128)S(1)}, f32[32,512,128]{2,1,0:T(8,128)S(1)}, f32[2,4,64,128]{3,2,1,0:T(8,128)}, f32[2,4,64,128]{3,2,1,0:T(8,128)S(1)}, f...) custom-call(f32[32,512,128]{2,1,0:T(8,128)} %bitcast.5, f32[32,512,128]{2,1,0:T(8,128)} %bitcast.6, ...), custom_call_target="tpu_custom_call" | custom-call | tf_op jit(solution)/shard_map/swap/pallas_call | solution.py:725
  319.5 0.6 collective-permute-start
  320.1 5.9 %emit.1 = (f32[32,512,128]{2,1,0:T(8,128)}, f32[32,512,128]{2,1,0:T(8,128)}) custom-call(f32[32,512,128]{2,1,0:T(8,128)S(1)} %get-tuple-element.16.heat, f32[32,512,128]{2,1,0:T(8,128)S(1)} %get-tuple-element.17.scored), custom_call_target="tpu_custom_call" | custom-call | flops 60000000 | bytes 33554432 | tf_op jit(solution)/shard_map/emit/pallas_call | solution.py:890
  326.0 1.0 collective-permute-done.far
  327.0 1.5 seam.1
Async XLA Ops:
  319.5 7.5 %collective-permute-start = (f32[2,4,64,128]{3,2,1,0:T(8,128)}, f32[2,4,64,128]{3,2,1,0:T(8,128)S(1)}, u32[]{:S(2)}, u32[]{:S(2)}) collective-permute-start(f32[2,4,64,128]{3,2,1,0:T(8,128)} %get-tuple-element.12), channel_id=1, source_target_pairs={{0,1},{1,0},{2,3},{3,2},{4,5},{5,4},{6,7},{7,6},{8,9},{9,8},{10,11... | collective-permute-start | bytes 786440 | tf_op jit(solution)/shard_map/ppermute | solution.py:887

commit v5 on v4

--- a/solution.py
+++ b/solution.py
@@ -242,7 +242,7 @@
     field, rim, core, ratio_far, forcing_far, back, stage,
     xsend, xrecv, csend, crecv, ends, ends_far, stats,
     load_sem, send_sem, ysend_sem, scale_recv, rim_recv, inner_recv, ends_recv, outer_recv,
-    xrecv_sem, yrecv_sem, cxrecv_sem, cyrecv_sem, stat_recv, seam_sem,
+    xrecv_sem, yrecv_sem, cxrecv_sem, cyrecv_sem, stat_recv, seam_sem, hello,
 ):
     depth, width, height = sizes
     half, planes, inside = width // 2, 2 * height, height - 2
@@ -394,15 +394,31 @@
         load(1, c, side).wait()
         split_into(ratio, 1, side, c)
 
-        @pl.when((u == 0) & (side == 0))
-        def _():
-            pl.semaphore_wait(barrier, len(greeted))
+        @pl.when((u == 0) & (side == 0) & jnp.logical_not(upper))
+        def _():
+            pl.semaphore_wait(barrier, 1)
+            pl.semaphore_signal(hello.at[0], inc=1, device_id=partner, device_id_type=MESH)
+
+        @pl.when((u == 0) & (side == 0) & upper)
+        def _():
+            pl.semaphore_wait(hello.at[0], 1)
+            for device in around:
+                pl.semaphore_signal(barrier, inc=1, device_id=device, device_id_type=MESH)
 
         ratio_copy(u, rows_of(c)).start()
         load(0, c, side).wait()
         split_heat(u, side, c)
         for end in (0, 1):
             rim_copy(end, u, c).start()
+
+        @pl.when((u == 0) & (side == 1) & upper)
+        def _():
+            pl.semaphore_wait(barrier, len(around))
+            pl.semaphore_signal(hello.at[1], inc=1, device_id=partner, device_id_type=MESH)
+
+        @pl.when((u == 0) & (side == 1) & jnp.logical_not(upper))
+        def _():
+            pl.semaphore_wait(hello.at[1], 1)
 
         @pl.when(side == 1)
         def _():
@@ -461,10 +477,13 @@
         forcing_copy(u, rows_of(c)).start()
 
     barrier = pltpu.get_barrier_semaphore()
-    greeted = [partner, beside("lat", -1), beside("lat", 1)]
-    greeted += [beside("lon", offset) for offset in range(1, counts["lon"])]
-    for device in greeted:
-        pl.semaphore_signal(barrier, inc=1, device_id=device, device_id_type=MESH)
+    around = [beside("lat", -1), beside("lat", 1)]
+    around += [beside("lon", offset) for offset in range(1, counts["lon"])]
+
+    @pl.when(upper)
+    def _():
+        pl.semaphore_signal(barrier, inc=1, device_id=partner, device_id_type=MESH)
+
     for side in (0, 1):
         for kind in (1, 0, 2):
             load(kind, chunk_of(0, side), side).start()
@@ -561,9 +580,8 @@
                 line = field[STEPS % 2, whose * height + end * (height - 1), row_of(u, k) + 1, inner, :]
                 mean = both_halves(jnp.sum(line, axis=0, keepdims=True)) * (1.0 / width)
                 centred = line - mean
-                ends[whose, u, 0, pl.ds(2 * k + end, 1), :] = mean
                 squares = both_halves(jnp.sum(centred * centred, axis=0, keepdims=True))
-                ends[whose, u, 1, pl.ds(2 * k + end, 1), :] = squares
+                ends[whose, u, pl.ds(2 * k + end, 1), :] = jnp.where(first_lanes(mean.shape), mean, squares)
 
     def both_halves(sums):
         tall = jnp.broadcast_to(sums, (8, sums.shape[1]))
@@ -643,10 +661,10 @@
             stats[0, u, 1, pl.ds(k * height + z, 1), :] = jnp.sum(centred * centred, axis=0, keepdims=True)
 
     def share_moments(u):
-        mask = first_lanes(ends_far.shape[2:])
-        for kind in (0, 1):
-            mine, far = ends[0, u, kind], ends_far[u, kind]
-            lines = jnp.where(upper, jnp.where(mask, far, mine), jnp.where(mask, mine, far))
+        mask = first_lanes(ends_far.shape[1:])
+        mine, far = ends[0, u], ends_far[u]
+        one, two = jnp.where(upper, far, mine), jnp.where(upper, mine, far)
+        for kind, lines in ((0, jnp.where(mask, one, turned(two))), (1, jnp.where(mask, turned(one), two))):
             for k in range(2 * rows):
                 for end in (0, 1):
                     at = k * height + end * (height - 1)
@@ -741,11 +759,11 @@
             vmem(3, 2, rows, width * height),
             vmem(STEPS, units, 2, 2 * rows, 2 * height), vmem(STEPS, units, 2, 2 * rows, 2 * height),
             vmem(units, 2, 2 * rows, 8), vmem(units, 2, 2 * rows, 8),
-            vmem(2, units, 2, 4 * rows), vmem(units, 2, 4 * rows),
+            vmem(2, units, 4 * rows), vmem(units, 4 * rows),
             vmem(lon, units, 2, 2 * rows * height),
             dma((3, 2)), dma((10,)), dma((2,)),
             dma((units,)), dma((units,)), dma((units,)), dma((units,)), dma((units,)),
-            dma((2, units)), dma((2,)), dma((units,)), dma((1,)), dma((2,)), dma((2,)),
+            dma((2, units)), dma((2,)), dma((units,)), dma((1,)), dma((2,)), dma((2,)), pltpu.SemaphoreType.REGULAR((2,)),
         ],
         compiler_params=pltpu.CompilerParams(
             collective_id=1, has_side_effects=True, vmem_limit_bytes=46 * 1024 * 1024

time: 329 us -> 327 us (level)
  no operation moved by 1% of the time
where the time goes in v5:
time: 327 us
  Pallas kernels  325 us (99%)
    pallas_call x1, Pallas kernels, swap(): pl.pallas_call(functools.partial(swap_kernel, sizes, rows), out_shape=(pl...  318 us
  transfers between devices with their start and end apart: 1, of which 1 were waited for; matrix products, arithmetic and copies ran while one was open for 0% of the time, Pallas kernels for 2%

profile of v5, /device:TPU:0, one launch (start us, length us, event | category | flops | bytes accessed | tf_op | source)
XLA Modules:
  0.0 326.8 jit_solution(12963234290968201567)
XLA Ops:
  0.6 318.0 %swap.1 = (f32[32,512,128]{2,1,0:T(8,128)S(1)}, f32[32,512,128]{2,1,0:T(8,128)S(1)}, f32[2,4,64,128]{3,2,1,0:T(8,128)}, f32[2,4,64,128]{3,2,1,0:T(8,128)S(1)}, f...) custom-call(f32[32,512,128]{2,1,0:T(8,128)} %bitcast.5, f32[32,512,128]{2,1,0:T(8,128)} %bitcast.6, ...), custom_call_target="tpu_custom_call" | custom-call | tf_op jit(solution)/shard_map/swap/pallas_call | solution.py:743
  318.7 0.1 collective-permute-start
  318.7 5.9 %emit.1 = (f32[32,512,128]{2,1,0:T(8,128)}, f32[32,512,128]{2,1,0:T(8,128)}) custom-call(f32[32,512,128]{2,1,0:T(8,128)S(1)} %get-tuple-element.16.heat, f32[32,512,128]{2,1,0:T(8,128)S(1)} %get-tuple-element.17.scored), custom_call_target="tpu_custom_call" | custom-call | flops 60000000 | bytes 33554432 | tf_op jit(solution)/shard_map/emit/pallas_call | solution.py:908
  324.7 0.6 collective-permute-done.far
  325.3 1.5 seam.1
Async XLA Ops:
  318.7 6.6 %collective-permute-start = (f32[2,4,64,128]{3,2,1,0:T(8,128)}, f32[2,4,64,128]{3,2,1,0:T(8,128)S(1)}, u32[]{:S(2)}, u32[]{:S(2)}) collective-permute-start(f32[2,4,64,128]{3,2,1,0:T(8,128)} %get-tuple-element.12), channel_id=1, source_target_pairs={{0,1},{1,0},{2,3},{3,2},{4,5},{5,4},{6,7},{7,6},{8,9},{9,8},{10,11... | collective-permute-start | bytes 786440 | tf_op jit(solution)/shard_map/ppermute | solution.py:905

commit v6 on v5

--- a/solution.py
+++ b/solution.py
@@ -807,11 +807,10 @@
     )(*arrays)
 
 
-def copy_kernel(chunks, heat, scored, score, end, sem):
-    rows = heat.shape[0] // chunks
+def copy_kernel(spans, heat, scored, score, end, sem):
     copies = []
-    for c in range(chunks):
-        span = pl.ds(c * rows, rows)
+    for c, (first, rows) in enumerate(spans):
+        span = pl.ds(first, rows)
         copies.append(pltpu.make_async_copy(heat.at[span], end.at[span], sem.at[0, c]))
         copies.append(pltpu.make_async_copy(scored.at[span], score.at[span], sem.at[1, c]))
     for copy in copies:
@@ -903,18 +902,20 @@
     if swaps:
         heat, scored, far, near, seam_rows, moments = swap(sizes, arrays)
         far = lax.ppermute(far, "lev", [(0, 1), (1, 0)])
-        parts = min(4, depth)
+        taken = seam_rows.shape[0]
+        first = (depth - taken) // 2
+        fourth = first // 2
+        spans = [(at + i * fourth, fourth + i * (first - 2 * fourth)) for at in (0, first + taken) for i in (0, 1)]
         in_hbm = pl.BlockSpec(memory_space=pltpu.HBM)
         score, end = pl.pallas_call(
-            functools.partial(copy_kernel, parts), out_shape=common["out_shape"], out_specs=(in_hbm,) * 2,
-            in_specs=inputs, scratch_shapes=[dma((2, parts))],
+            functools.partial(copy_kernel, spans), out_shape=common["out_shape"], out_specs=(in_hbm,) * 2,
+            in_specs=inputs, scratch_shapes=[dma((2, len(spans)))],
             cost_estimate=pl.CostEstimate(flops=60000000, bytes_accessed=4 * heat.nbytes, transcendentals=0),
             compiler_params=pltpu.CompilerParams(vmem_limit_bytes=8 * 1024 * 1024),
             name="emit",
         )(heat, scored)
-        taken = seam_rows.shape[0]
         score, end = pl.pallas_call(
-            functools.partial(seam_kernel, (width, height, (depth - taken) // 2)),
+            functools.partial(seam_kernel, (width, height, first)),
             out_shape=common["out_shape"], out_specs=(in_hbm,) * 2,
             in_specs=[pl.BlockSpec(memory_space=pltpu.VMEM)] * 4 + [in_hbm] * 2,
             scratch_shapes=[pltpu.VMEM(seam_rows.shape, f32)] * 2 + [dma((2, taken))],

time: 327 us -> 327 us (level)
  no operation moved by 1% of the time
where the time goes in v6:
time: 327 us
  Pallas kernels  325 us (99%)
    pallas_call x1, Pallas kernels, swap(): pl.pallas_call(functools.partial(swap_kernel, sizes, rows), out_shape=(pl...  318 us
  transfers between devices with their start and end apart: 1, of which 1 were waited for; matrix products, arithmetic and copies ran while one was open for 0% of the time, Pallas kernels for 2%

profile of v6, /device:TPU:0, one launch (start us, length us, event | category | flops | bytes accessed | tf_op | source)
XLA Modules:
  0.0 326.8 jit_solution(1459809942574790631)
XLA Ops:
  0.6 318.0 %swap.1 = (f32[32,512,128]{2,1,0:T(8,128)S(1)}, f32[32,512,128]{2,1,0:T(8,128)S(1)}, f32[2,4,64,128]{3,2,1,0:T(8,128)}, f32[2,4,64,128]{3,2,1,0:T(8,128)S(1)}, f...) custom-call(f32[32,512,128]{2,1,0:T(8,128)} %bitcast.5, f32[32,512,128]{2,1,0:T(8,128)} %bitcast.6, ...), custom_call_target="tpu_custom_call" | custom-call | tf_op jit(solution)/shard_map/swap/pallas_call | solution.py:743
  318.7 0.1 collective-permute-start
  318.7 5.3 %emit.1 = (f32[32,512,128]{2,1,0:T(8,128)}, f32[32,512,128]{2,1,0:T(8,128)}) custom-call(f32[32,512,128]{2,1,0:T(8,128)S(1)} %get-tuple-element.16.heat, f32[32,512,128]{2,1,0:T(8,128)S(1)} %get-tuple-element.17.scored), custom_call_target="tpu_custom_call" | custom-call | flops 60000000 | bytes 33554432 | tf_op jit(solution)/shard_map/emit/pallas_call | solution.py:910
  324.1 1.2 collective-permute-done.far
  325.3 1.5 seam.1
Async XLA Ops:
  318.7 6.6 %collective-permute-start = (f32[2,4,64,128]{3,2,1,0:T(8,128)}, f32[2,4,64,128]{3,2,1,0:T(8,128)S(1)}, u32[]{:S(2)}, u32[]{:S(2)}) collective-permute-start(f32[2,4,64,128]{3,2,1,0:T(8,128)} %get-tuple-element.12), channel_id=1, source_target_pairs={{0,1},{1,0},{2,3},{3,2},{4,5},{5,4},{6,7},{7,6},{8,9},{9,8},{10,11... | collective-permute-start | bytes 786440 | tf_op jit(solution)/shard_map/ppermute | solution.py:904
